TPU v7x, 32 devices: a whole 2x2x4 slice. The times are simulated.
32 devices in a mesh: dp: 2 (over core), mp: 16 (over z, y, x).
Axes of the slice: x: 2, y: 2, z: 4, core: 2. Of those that a mesh axis runs over, the one named last changes fastest.
Arguments:
- tokens: bfloat16 [512, 2048], P('dp', 'mp'), may hold values from -6 to 6
- gate_weights: bfloat16 [2, 2048, 7168], P(None, None, 'mp'), may hold values from -0.125 to 0.125
- up_weights: bfloat16 [2, 2048, 7168], P(None, None, 'mp'), may hold values from -0.125 to 0.125
- down_weights: bfloat16 [2, 7168, 2048], P(None, 'mp'), may hold values from -0.0625 to 0.0625
- rhs_gate: float32 [2, 2048, 7168], P(None, 'dp', 'mp'), may hold values from -6 to 6
- rhs_up: float32 [2, 2048, 7168], P(None, 'dp', 'mp'), may hold values from -6 to 6
- rhs_down: float32 [2, 7168, 2048], P(None, 'mp', 'dp'), may hold values from -6 to 6
- damping: float32 [1], replicated, may hold values from 0.5 to 2
Outputs:
- step_gate: float32 [2, 2048, 7168], P(None, 'dp', 'mp')
- step_up: float32 [2, 2048, 7168], P(None, 'dp', 'mp')
- step_down: float32 [2, 7168, 2048], P(None, 'mp', 'dp')
- next_gate: float32 [2, 2048, 7168], P(None, 'dp', 'mp')
- next_up: float32 [2, 2048, 7168], P(None, 'dp', 'mp')
- next_down: float32 [2, 7168, 2048], P(None, 'mp', 'dp')
All inputs are finite; a program needn't handle non-finite values.
Results may differ from a plain program's by a relative error of at most 0.007.
Values may be sent and summed in bfloat16 or wider, within the bound.
A program may use at most 128 MiB of HBM per device.

v0:
```python
import jax
import jax.numpy as jnp
from jax import lax
from jax.sharding import PartitionSpec as P

ITERS = 1


def silu_terms(value):
    sigmoid_value = jax.nn.sigmoid(value)
    return (value * sigmoid_value, sigmoid_value * (1.0 + value * (1.0 - sigmoid_value)))


def matmul(left, right):
    return jnp.dot(left, right, preferred_element_type=jnp.float32)


def rows_product(left, right):
    return lax.dot_general(
        left, right, (((0,), (0,)), ((), ())), preferred_element_type=jnp.float32
    )


def against(left, right):
    return lax.dot_general(
        left, right, (((1,), (1,)), ((), ())), preferred_element_type=jnp.float32
    )


def local_inner(first, second):
    return (
        jnp.sum(first[0] * second[0])
        + jnp.sum(first[1] * second[1])
        + jnp.sum(first[2] * second[2])
    )


def finish_first(partial_value, whole_add):
    summed = lax.psum(partial_value, "mp")
    if whole_add is not None:
        summed = summed + whole_add.astype(jnp.float32)
    return summed.astype(jnp.bfloat16)


def body(tokens, gate_weights, up_weights, down_weights, rhs_gate, rhs_up, rhs_down, damping):
    share = tokens.shape[1]
    offset = lax.axis_index("mp") * share
    total_tokens = tokens.shape[0] * lax.axis_size("dp")
    tokens_whole = lax.all_gather(tokens, "mp", axis=1, tiled=True)
    gate_one = matmul(tokens_whole, gate_weights[0])
    up_one = matmul(tokens_whole, up_weights[0])
    active_one, slope_one = silu_terms(gate_one)
    hidden_one = (active_one * up_one).astype(jnp.bfloat16)
    layer_one = finish_first(matmul(hidden_one, down_weights[0]), tokens_whole)
    gate_two = matmul(layer_one, gate_weights[1])
    up_two = matmul(layer_one, up_weights[1])
    active_two, slope_two = silu_terms(gate_two)
    hidden_two = (active_two * up_two).astype(jnp.bfloat16)

    def curvature(vectors):
        tangent_gate, tangent_up, tangent_down = (
            lax.all_gather(vectors[0].astype(jnp.bfloat16), "dp", axis=1, tiled=True),
            lax.all_gather(vectors[1].astype(jnp.bfloat16), "dp", axis=1, tiled=True),
            lax.all_gather(vectors[2].astype(jnp.bfloat16), "dp", axis=2, tiled=True),
        )
        tan_gate = matmul(tokens_whole, tangent_gate[0])
        tan_up = matmul(tokens_whole, tangent_up[0])
        tan_hidden = (slope_one * up_one * tan_gate + active_one * tan_up).astype(jnp.bfloat16)
        tan_layer = finish_first(
            matmul(tan_hidden, down_weights[0]) + matmul(hidden_one, tangent_down[0]), None
        )
        tan_gate = matmul(tan_layer, gate_weights[1]) + matmul(layer_one, tangent_gate[1])
        tan_up = matmul(tan_layer, up_weights[1]) + matmul(layer_one, tangent_up[1])
        tan_hidden = (slope_two * up_two * tan_gate + active_two * tan_up).astype(jnp.bfloat16)
        second_partial = matmul(tan_hidden, down_weights[1]) + matmul(hidden_two, tangent_down[1])
        second_summed = lax.psum_scatter(second_partial, "mp", scatter_dimension=1, tiled=True)
        layer_slice = lax.dynamic_slice_in_dim(tan_layer, offset, share, 1)
        cotan_share = (layer_slice.astype(jnp.float32) + second_summed).astype(jnp.bfloat16)
        cotan = lax.all_gather(cotan_share, "mp", axis=1, tiled=True)
        grad_down_two = rows_product(hidden_two, cotan)
        back_hidden = against(cotan, down_weights[1])
        back_gate = (back_hidden * up_two * slope_two).astype(jnp.bfloat16)
        back_up = (back_hidden * active_two).astype(jnp.bfloat16)
        grad_gate_two = rows_product(layer_one, back_gate)
        grad_up_two = rows_product(layer_one, back_up)
        back_partial = against(back_gate, gate_weights[1]) + against(back_up, up_weights[1])
        back_layer = finish_first(back_partial, cotan)
        grad_down_one = rows_product(hidden_one, back_layer)
        back_hidden = against(back_layer, down_weights[0])
        back_gate = (back_hidden * up_one * slope_one).astype(jnp.bfloat16)
        back_up = (back_hidden * active_one).astype(jnp.bfloat16)
        grad_gate_one = rows_product(tokens_whole, back_gate)
        grad_up_one = rows_product(tokens_whole, back_up)
        summed_gate, summed_up, summed_down = (
            lax.psum_scatter(
                jnp.stack([grad_gate_one, grad_gate_two]).astype(jnp.bfloat16),
                "dp",
                scatter_dimension=1,
                tiled=True,
            ).astype(jnp.float32),
            lax.psum_scatter(
                jnp.stack([grad_up_one, grad_up_two]).astype(jnp.bfloat16),
                "dp",
                scatter_dimension=1,
                tiled=True,
            ).astype(jnp.float32),
            lax.psum_scatter(
                jnp.stack([grad_down_one, grad_down_two]).astype(jnp.bfloat16),
                "dp",
                scatter_dimension=2,
                tiled=True,
            ).astype(jnp.float32),
        )
        scale = 1.0 / total_tokens
        return (
            summed_gate * scale + damping[0] * vectors[0],
            summed_up * scale + damping[0] * vectors[1],
            summed_down * scale + damping[0] * vectors[2],
        )

    residual = (rhs_gate, rhs_up, rhs_down)
    direction = residual
    solution = (jnp.zeros_like(rhs_gate), jnp.zeros_like(rhs_up), jnp.zeros_like(rhs_down))
    norm_now = lax.psum(local_inner(residual, residual), ("dp", "mp"))
    for rounds in range(ITERS):
        image = curvature(direction)
        along, crossed, squared = lax.psum(
            (
                local_inner(direction, image),
                local_inner(residual, image),
                local_inner(image, image),
            ),
            ("dp", "mp"),
        )
        alpha = norm_now / along
        solution = tuple((solution[k] + alpha * direction[k] for k in range(3)))
        residual = tuple((residual[k] - alpha * image[k] for k in range(3)))
        norm_next = norm_now - 2.0 * alpha * crossed + alpha * alpha * squared
        direction = tuple((residual[k] + norm_next / norm_now * direction[k] for k in range(3)))
        norm_now = norm_next
    return (solution[0], solution[1], solution[2], direction[0], direction[1], direction[2])


def solution(mesh):
    in_specs = (
        P("dp", "mp"),
        P(None, None, "mp"),
        P(None, None, "mp"),
        P(None, "mp", None),
        P(None, "dp", "mp"),
        P(None, "dp", "mp"),
        P(None, "mp", "dp"),
        P(),
    )
    out_specs = (
        P(None, "dp", "mp"),
        P(None, "dp", "mp"),
        P(None, "mp", "dp"),
        P(None, "dp", "mp"),
        P(None, "dp", "mp"),
        P(None, "mp", "dp"),
    )
    return jax.shard_map(body, mesh=mesh, in_specs=in_specs, out_specs=out_specs, check_vma=False)
```

profile of v0, /device:TPU:0, one launch (start us, length us, event | category | flops | bytes accessed | tf_op | source)
XLA Modules:
  0.0 681.3 jit_solution(4627766731937684603)
XLA Ops:
  7.9 3.6 convert_element_type.67
  11.6 3.6 convert_element_type.66
  15.2 3.6 convert_element_type.70
  18.8 49.8 %all-gather.6.cloned.1.call-done = bf16[256,2048]{1,0:T(8,128)(2,1)} async-done(((bf16[256,128]{1,0:T(8,128)(2,1)}), bf16[256,2048]{1,0:T(8,128)(2,1)}) %all-gather.6.cloned.1.call-update) | async-done | bytes 1048592 | tf_op jit(solution)/shard_map/all_gather | solution.py:49
  76.2 6.9 %all-gather.10.cloned.1.call-done = bf16[2,2048,448]{1,2,0:T(8,128)(2,1)} async-done(((bf16[2,1024,448]{1,2,0:T(8,128)(2,1)}), bf16[2,2048,448]{1,2,0:T(8,128)(2,1)}) %all-gather.10.cloned.1.call-update) | async-done | bytes 3670032 | tf_op jit(solution)/shard_map/all_gather | solution.py:63
  85.2 14.0 %all-gather.8.cloned.1.call-done = bf16[2,2048,448]{1,2,0:T(8,128)(2,1)} async-done(((bf16[2,1024,448]{1,2,0:T(8,128)(2,1)}), bf16[2,2048,448]{1,2,0:T(8,128)(2,1)}) %all-gather.8.cloned.1.call-update) | async-done | bytes 3670032 | tf_op jit(solution)/shard_map/all_gather | solution.py:62
  99.3 5.7 fusion.29
  104.9 10.4 %all-gather.12.cloned.1.call-done = bf16[2,448,2048]{2,1,0:T(8,128)(2,1)} async-done(((bf16[2,448,1024]{2,1,0:T(8,128)(2,1)}), bf16[2,448,2048]{2,1,0:T(8,128)(2,1)}) %all-gather.12.cloned.1.call-update) | async-done | bytes 3670032 | tf_op jit(solution)/shard_map/all_gather | solution.py:64
  118.2 112.4 %all-reduce.8 = bf16[256,2048]{1,0:T(8,128)(2,1)} all-reduce(f32[256,2048]{1,0:T(8,128)S(1)} %convolution_add_fusion.2), channel_id=1, replica_groups=mesh['dp'=2,'mp'=16] {'mp'}, use_global_device_ids=true, to_apply=%region_4.0 | all-reduce | flops 524288 | bytes 3145728 | tf_op jit(solution)/shard_map/psum | solution.py:39
  230.6 37.7 %all-reduce.5.cloned.1.call-done = f32[256,2048]{1,0:T(8,128)} async-done(((f32[256,2048]{1,0:T(8,128)}), f32[256,2048]{1,0:T(8,128)}) %all-reduce.5.cloned.1.call-update) | async-done | bytes 2097168 | tf_op jit(solution)/shard_map/psum | solution.py:39
  278.8 6.2 fusion.12
  285.1 4.3 convolution_add_fusion.1
  289.4 80.4 %reduce-scatter.5.cloned.1.call-done = f32[256,128]{1,0:T(8,128)} async-done(((f32[256,2048]{1,0:T(8,128)}), f32[256,128]{1,0:T(8,128)}) %reduce-scatter.5.cloned.1.call-update) | async-done | bytes 131088 | tf_op jit(solution)/shard_map/reduce_scatter | solution.py:76
  371.5 53.8 %all-gather.14.cloned.1.call-done = bf16[256,2048]{1,0:T(8,128)(2,1)} async-done(((bf16[256,128]{1,0:T(8,128)(2,1)}), bf16[256,2048]{1,0:T(8,128)(2,1)}) %all-gather.14.cloned.1.call-update) | async-done | bytes 1048592 | tf_op jit(solution)/shard_map/all_gather | solution.py:79
  435.5 123.4 %all-reduce.7.cloned.1.call-done = f32[256,2048]{1,0:T(8,128)} async-done(((f32[256,2048]{1,0:T(8,128)}), f32[256,2048]{1,0:T(8,128)}) %all-reduce.7.cloned.1.call-update) | async-done | bytes 2097168 | tf_op jit(solution)/shard_map/psum | solution.py:39
  558.9 3.0 fusion.25
  578.1 4.4 multiply_reduce_fusion.2
  582.5 9.7 %reduce-scatter.9.cloned.1.call-done = bf16[2,1024,448]{1,2,0:T(8,128)(2,1)} async-done(((bf16[2,2048,448]{1,2,0:T(8,128)(2,1)}), bf16[2,1024,448]{1,2,0:T(8,128)(2,1)}) %reduce-scatter.9.cloned.1.call-update) | async-done | bytes 1835024 | tf_op jit(solution)/shard_map/reduce_scatter | solution.py:101
  592.2 4.4 multiply_reduce_fusion.1
  598.0 10.0 %reduce-scatter.11.cloned.1.call-done = bf16[2,448,1024]{2,1,0:T(8,128)(2,1)} async-done(((bf16[2,448,2048]{2,1,0:T(8,128)(2,1)}), bf16[2,448,1024]{2,1,0:T(8,128)(2,1)}) %reduce-scatter.11.cloned.1.call-update) | async-done | bytes 1835024 | tf_op jit(solution)/shard_map/reduce_scatter | solution.py:107
  608.0 4.4 multiply_reduce_fusion
  616.9 40.6 %all-reduce = (f32[]{:T(128)}, f32[]{:T(128)}, f32[]{:T(128)}) all-reduce(f32[]{:T(128)S(6)} %add.108, f32[]{:T(128)S(6)} %add.128, f32[]{:T(128)S(6)} %add.130), channel_id=1, replica_groups=mesh['dp'=2,'mp'=16] {'dp','mp'}, use_global_device_ids=true, to_apply=%region_3.0 | all-reduce | flops 3 | bytes 24 | tf_op jit(solution)/shard_map/psum | solution.py:124
  661.5 9.2 %multiply_add_fusion.1 = (f32[2,1024,448]{1,2,0:T(8,128)}, f32[2,1024,448]{1,2,0:T(8,128)}, f32[2,1024,448]{1,2,0:T(8,128)}, f32[2,1024,448]{1,2,0:T(8,128)}) fusion(f32[2,1024,448]{1,2,0:T(8,128)} %param.13, bf16[2,1024,448]{1,2,0:T(8,128)(2,1)} %reduce-scatter.9.cloned.1.call-done, f32[]{:T(128)S(6)} %div.17, f32[]{:T(128)S(6)} %div.16, f32[]{:T(128)} %bitcast.123, ...), kind=kLoop, calls=%fused_computation.4 | loop fusion | flops 16515072 | bytes 25690124 | tf_op jit(solution)/shard_map/add | solution.py:139
  670.7 4.1 multiply_add_fusion
  (93 shorter events, 51.3 us)
Async XLA Ops:
  7.2 61.5 %all-gather.6.cloned.1.call-start = ((), (), s32[]{:S(2)}) async-start(), calls=%async_computation.4 | async-start | bytes 1114112 | tf_op jit(solution)/shard_map/all_gather | solution.py:49
  7.9 75.1 %all-gather.10.cloned.1.call-start = ((), (), s32[]{:S(2)}) async-start(), calls=%async_computation.6 | async-start | bytes 5505024 | tf_op jit(solution)/shard_map/all_gather | solution.py:63
  11.5 87.7 %all-gather.8.cloned.1.call-start = ((), (), s32[]{:S(2)}) async-start(), calls=%async_computation.5 | async-start | bytes 5505024 | tf_op jit(solution)/shard_map/all_gather | solution.py:62
  15.2 100.2 %all-gather.12.cloned.1.call-start = ((), (), s32[]{:S(2)}) async-start(), calls=%async_computation.7 | async-start | bytes 5505024 | tf_op jit(solution)/shard_map/all_gather | solution.py:64
  18.8 249.5 %all-reduce.5.cloned.1.call-start = ((), (), s32[]{:S(2)}) async-start(), calls=%async_computation.8 | async-start | bytes 4194304 | tf_op jit(solution)/shard_map/psum | solution.py:39
  71.3 28.0 %copy-start.8 = (f32[256,448]{0,1:T(8,128)}, f32[256,448]{0,1:T(8,128)S(1)}, u32[]{:S(2)}) copy-start(f32[256,448]{0,1:T(8,128)S(1)} %fusion.33) | copy-start | bytes 1376260
  73.7 25.6 %copy-start.18 = (f32[256,448]{0,1:T(8,128)}, f32[256,448]{0,1:T(8,128)S(1)}, u32[]{:S(2)}) copy-start(f32[256,448]{0,1:T(8,128)S(1)} %get-tuple-element.27) | copy-start | bytes 1376260
  76.1 293.7 %reduce-scatter.5.cloned.1.call-start = ((), (), s32[]{:S(2)}) async-start(), calls=%async_computation.9 | async-start | bytes 2228224 | tf_op jit(solution)/shard_map/reduce_scatter | solution.py:76
  268.3 3.8 copy-start.16
  272.0 3.1 copy-start.22
  272.0 3.1 copy-start.10
  289.4 135.9 %all-gather.14.cloned.1.call-start = ((), (), s32[]{:S(2)}) async-start(), calls=%async_computation.10 | async-start | bytes 1114112 | tf_op jit(solution)/shard_map/all_gather | solution.py:79
  371.4 187.4 %all-reduce.7.cloned.1.call-start = ((), (), s32[]{:S(2)}) async-start(), calls=%async_computation.11 | async-start | bytes 4194304 | tf_op jit(solution)/shard_map/psum | solution.py:39
  425.3 3.2 copy-start.15
  432.5 126.3 %copy-start.1 = (bf16[256,2048]{1,0:T(8,128)(2,1)S(1)}, bf16[256,2048]{1,0:T(8,128)(2,1)}, u32[]{:S(2)}) copy-start(bf16[256,2048]{1,0:T(8,128)(2,1)} %all-gather.14.cloned.1.call-done) | copy-start | bytes 3145732
  432.5 145.5 %reduce-scatter.7.cloned.1.call-start = ((), (), s32[]{:S(2)}) async-start(), calls=%async_computation.12 | async-start | bytes 5505024 | tf_op jit(solution)/shard_map/reduce_scatter | solution.py:95
  558.8 3.8 copy-start.9
  558.9 3.8 copy-start.19
  558.9 4.5 copy-start.4
  565.5 26.7 %reduce-scatter.9.cloned.1.call-start = ((), (), s32[]{:S(2)}) async-start(), calls=%async_computation.13 | async-start | bytes 5505024 | tf_op jit(solution)/shard_map/reduce_scatter | solution.py:101
  571.4 36.6 %reduce-scatter.11.cloned.1.call-start = ((), (), s32[]{:S(2)}) async-start(), calls=%async_computation.14 | async-start | bytes 5505024 | tf_op jit(solution)/shard_map/reduce_scatter | solution.py:107
  596.6 64.8 %copy-start.3 = (bf16[2,1024,448]{1,2,0:T(8,128)(2,1)S(1)}, bf16[2,1024,448]{1,2,0:T(8,128)(2,1)}, u32[]{:S(2)}) copy-start(bf16[2,1024,448]{1,2,0:T(8,128)(2,1)} %reduce-scatter.7.cloned.1.call-done) | copy-start | bytes 5505028
  661.5 9.2 %copy-start = (f32[2,448,1024]{2,1,0:T(8,128)S(1)}, f32[2,448,1024]{2,1,0:T(8,128)}, u32[]{:S(2)}) copy-start(f32[2,448,1024]{2,1,0:T(8,128)} %param.14) | copy-start | bytes 11010052
  661.5 9.2 %copy-start.5 = (bf16[2,448,1024]{2,1,0:T(8,128)(2,1)S(1)}, bf16[2,448,1024]{2,1,0:T(8,128)(2,1)}, u32[]{:S(2)}) copy-start(bf16[2,448,1024]{2,1,0:T(8,128)(2,1)} %reduce-scatter.11.cloned.1.call-done) | copy-start | bytes 5505028
  (10 other events, 18.7 us)
Sparse Core Ops, SparseCore 0:
  10.7 57.9 all-gather.5
  70.8 12.1 all-gather.9
  85.2 14.0 all-gather.7
  101.2 14.0 all-gather.11
  121.2 146.9 all-reduce.4
  289.5 80.3 reduce-scatter.4
  373.1 52.1 all-gather.13
  432.7 126.1 all-reduce.6
  565.7 10.8 reduce-scatter.6
  579.3 12.8 reduce-scatter.8
  595.0 12.8 reduce-scatter.10
where the time goes:
time: 682 us; the launch traced here: 681 us
  waiting for transfers between devices  397 us (58%)
  blocking collectives  153 us (22%)
  matrix products  52.5 us (8%)
  other arithmetic  47.2 us (7%)
  between operations  24.7 us (4%)
    psum x2, waiting for transfers between devices, finish_first(): summed = lax.psum(partial_value, 'mp')  161 us
    psum x1, blocking collectives, finish_first(): summed = lax.psum(partial_value, 'mp')  112 us
    reduce_scatter x1, waiting for transfers between devices, curvature(): lax.psum_scatter(second_partial, 'mp', scatter_dimension=1, tiled=True)  80.4 us
    all_gather x1, waiting for transfers between devices, curvature(): cotan = lax.all_gather(cotan_share, 'mp', axis=1, tiled=True)  53.8 us
    all_gather x1, waiting for transfers between devices, body(): tokens_whole = lax.all_gather(tokens, 'mp', axis=1, tiled=True)  49.8 us
    psum x1, blocking collectives, body(): norm_now = lax.psum(local_inner(residual, residual), ('dp', 'mp'))  40.6 us
    dot_general x13, matrix products, matmul(): return jnp.dot(left, right, preferred_element_type=jnp.float32)  34 us
    all_gather x1, waiting for transfers between devices, curvature(): lax.all_gather(vectors[0].astype(jnp.bfloat16), 'dp', axis=1, tiled=True)  14 us
  transfers between devices with their start and end apart: 11, of which 10 were waited for; matrix products, arithmetic and copies ran while one was open for 7% of the time, Pallas kernels for 0%

commit v1 on v0

v1 whole, which is shorter than its diff:
```python
import functools
import jax
import jax.numpy as jnp
from jax import lax
from jax.experimental import pallas as pl
from jax.experimental.pallas import tpu as pltpu
from jax.sharding import PartitionSpec as P

ITERS = 1
MESH = pl.DeviceIdType.MESH


def split_of(count):
    inner = 1
    while inner * inner < count and count % (inner * 2) == 0:
        inner *= 2
    return count // inner, inner


def greet(peers):
    barrier = pltpu.get_barrier_semaphore()
    for peer in peers:
        pl.semaphore_signal(barrier, inc=1, device_id=peer, device_id_type=MESH)
    pl.semaphore_wait(barrier, len(peers))


def place(outer, inner):
    me = lax.axis_index("mp")
    far, near = lax.div(me, inner), lax.rem(me, inner)

    def along_outer(step):
        return {"mp": lax.rem(far + step, outer) * inner + near}

    def along_inner(step):
        return {"mp": far * inner + lax.rem(near + step, inner)}

    return far, near, along_outer, along_inner


def remote(source, target, send, receive, peer):
    copy = pltpu.make_async_remote_copy(
        src_ref=source, dst_ref=target, send_sem=send, recv_sem=receive,
        device_id=peer, device_id_type=MESH,
    )
    copy.start()
    return copy


def sum_kernel(outer, inner, count, adds, *refs):
    parts = refs[:count]
    extra = dict(zip(adds, refs[count:count + len(adds)]))
    outs = refs[count + len(adds):2 * count + len(adds)]
    near_slots, held, far_slots, s1s, s1r, s2s, s2r, g1s, g1r, g2s, g2r = refs[2 * count + len(adds):]
    far, near, along_outer, along_inner = place(outer, inner)
    greet([along_outer(e) for e in range(1, outer)] + [along_inner(d) for d in range(1, inner)])
    order = list(range(1, outer)) + [0]
    copies = []
    first, second, third, fourth = {}, {}, {}, {}
    for e in order:
        piece = lax.rem(far + e, outer)
        for k in range(count):
            for d in range(1, inner):
                first[k, d, e] = remote(
                    parts[k].at[lax.rem(near + d, inner), piece], near_slots.at[k, d, e],
                    s1s.at[k, d, e], s1r.at[k, d, e], along_inner(d),
                )
    own = {}
    for e in order:
        piece = lax.rem(far + e, outer)
        for k in range(count):
            total = parts[k][near, piece].astype(jnp.float32)
            for d in range(1, inner):
                first[k, d, e].wait_recv()
                total = total + near_slots[k, d, e].astype(jnp.float32)
            if e:
                held[k, e] = total.astype(jnp.bfloat16)
                second[k, e] = remote(
                    held.at[k, e], far_slots.at[k, e], s2s.at[k, e], s2r.at[k, e], along_outer(e)
                )
            else:
                own[k] = total
    for k in range(count):
        total = own[k]
        for e in range(1, outer):
            second[k, e].wait_recv()
            total = total + far_slots[k, e].astype(jnp.float32)
        if k in extra:
            total = total + extra[k][near, far].astype(jnp.float32)
        outs[k][near, far] = total.astype(jnp.bfloat16)
        spread(outer, inner, outs[k], far, near, along_outer, along_inner, third, fourth, k,
               g1s, g1r, g2s, g2r)
    forward(outer, inner, outs, far, near, along_inner, third, fourth, g2s, g2r)
    for table in (first, second, third, fourth):
        for copy in table.values():
            copy.wait_send()


def spread(outer, inner, out, far, near, along_outer, along_inner, third, fourth, k, g1s, g1r, g2s, g2r):
    for e in range(1, outer):
        third[k, e] = remote(out.at[near, far], out.at[near, far], g1s.at[k, e], g1r.at[k, e], along_outer(e))
    for d in range(1, inner):
        fourth[k, d, 0] = remote(
            out.at[near, far], out.at[near, far], g2s.at[k, d, 0], g2r.at[k, d, 0], along_inner(d)
        )


def forward(outer, inner, outs, far, near, along_inner, third, fourth, g2s, g2r):
    for e in range(1, outer):
        piece = lax.rem(far - e + outer, outer)
        for k in range(len(outs)):
            third[k, e].wait_recv()
            for d in range(1, inner):
                fourth[k, d, e] = remote(
                    outs[k].at[near, piece], outs[k].at[near, piece],
                    g2s.at[k, d, e], g2r.at[k, d, e], along_inner(d),
                )
    for copy in fourth.values():
        copy.wait_recv()


def summed_whole(mp, parts, adds, ident):
    outer, inner = split_of(mp)
    rows, width = parts[0].shape
    share = rows // mp
    count = len(parts)
    view = (inner, outer, share, width)
    which = tuple(k for k in range(count) if adds[k] is not None)
    operands = [p.astype(jnp.bfloat16).reshape(view) for p in parts]
    operands += [adds[k].reshape(view) for k in which]
    dma = pltpu.SemaphoreType.DMA
    outs = pl.pallas_call(
        functools.partial(sum_kernel, outer, inner, count, which),
        out_shape=[jax.ShapeDtypeStruct(view, jnp.bfloat16)] * count,
        in_specs=[pl.BlockSpec(memory_space=pltpu.VMEM)] * len(operands),
        out_specs=[pl.BlockSpec(memory_space=pltpu.VMEM)] * count,
        scratch_shapes=[
            pltpu.VMEM((count, inner, outer, share, width), jnp.bfloat16),
            pltpu.VMEM((count, outer, share, width), jnp.bfloat16),
            pltpu.VMEM((count, outer, share, width), jnp.bfloat16),
            dma((count, inner, outer)), dma((count, inner, outer)),
            dma((count, outer)), dma((count, outer)),
            dma((count, outer)), dma((count, outer)),
            dma((count, inner, outer)), dma((count, inner, outer)),
        ],
        cost_estimate=pl.CostEstimate(
            flops=0, bytes_accessed=count * rows * width * 64, transcendentals=0
        ),
        compiler_params=pltpu.CompilerParams(collective_id=ident, has_side_effects=True),
    )(*operands)
    return [o.reshape(rows, width) for o in outs]


def gather_kernel(outer, inner, mine, out, local, g1s, g1r, g2s, g2r):
    far, near, along_outer, along_inner = place(outer, inner)
    greet([along_outer(e) for e in range(1, outer)] + [along_inner(d) for d in range(1, inner)])
    third, fourth = {}, {}
    keep = pltpu.make_async_copy(mine, out.at[far, near], local)
    keep.start()
    for e in range(1, outer):
        third[e] = remote(mine, out.at[far, near], g1s.at[e], g1r.at[e], along_outer(e))
    for d in range(1, inner):
        fourth[d, 0] = remote(mine, out.at[far, near], g2s.at[d, 0], g2r.at[d, 0], along_inner(d))
    for e in range(1, outer):
        piece = lax.rem(far - e + outer, outer)
        third[e].wait_recv()
        for d in range(1, inner):
            fourth[d, e] = remote(
                out.at[piece, near], out.at[piece, near], g2s.at[d, e], g2r.at[d, e], along_inner(d)
            )
    for copy in fourth.values():
        copy.wait_recv()
    keep.wait()
    for table in (third, fourth):
        for copy in table.values():
            copy.wait_send()


def gathered(mp, tokens, ident):
    outer, inner = split_of(mp)
    rows, share = tokens.shape
    dma = pltpu.SemaphoreType.DMA
    out = pl.pallas_call(
        functools.partial(gather_kernel, outer, inner),
        out_shape=jax.ShapeDtypeStruct((outer, inner, rows, share), tokens.dtype),
        in_specs=[pl.BlockSpec(memory_space=pltpu.VMEM)],
        out_specs=pl.BlockSpec(memory_space=pltpu.VMEM),
        scratch_shapes=[dma, dma((outer,)), dma((outer,)), dma((inner, outer)), dma((inner, outer))],
        cost_estimate=pl.CostEstimate(
            flops=0, bytes_accessed=rows * share * mp * 32, transcendentals=0
        ),
        compiler_params=pltpu.CompilerParams(collective_id=ident, has_side_effects=True),
    )(tokens)
    return out.reshape(mp, rows, share).transpose(1, 0, 2).reshape(rows, mp * share)


def scalar_kernel(dp, mp, mine, out, slots, send, receive):
    row, column = lax.axis_index("dp"), lax.axis_index("mp")
    total = dp * mp
    me = row * mp + column

    def other(step):
        index = lax.rem(me + step, total)
        return {"dp": lax.div(index, mp), "mp": lax.rem(index, mp)}

    greet([other(step) for step in range(1, total)])
    copies = [
        remote(mine, slots.at[me], send.at[step], receive.at[step], other(step))
        for step in range(1, total)
    ]
    slots[me] = mine[...]
    for copy in copies:
        copy.wait_recv()
    out[...] = jnp.sum(slots[...], axis=0)
    for copy in copies:
        copy.wait_send()


def scalars_summed(dp, mp, values, ident):
    packed = jnp.stack(values)
    packed = jnp.pad(packed, (0, 128 - len(values)))
    packed = jnp.broadcast_to(packed[None], (8, 128))
    total = dp * mp
    dma = pltpu.SemaphoreType.DMA
    out = pl.pallas_call(
        functools.partial(scalar_kernel, dp, mp),
        out_shape=jax.ShapeDtypeStruct((8, 128), jnp.float32),
        in_specs=[pl.BlockSpec(memory_space=pltpu.VMEM)],
        out_specs=pl.BlockSpec(memory_space=pltpu.VMEM),
        scratch_shapes=[pltpu.VMEM((total, 8, 128), jnp.float32), dma((total,)), dma((total,))],
        compiler_params=pltpu.CompilerParams(collective_id=ident, has_side_effects=True),
    )(packed)
    return [out[0, k] for k in range(len(values))]


def silu_terms(value):
    sigmoid_value = jax.nn.sigmoid(value)
    return (value * sigmoid_value, sigmoid_value * (1.0 + value * (1.0 - sigmoid_value)))


def matmul(left, right):
    return jnp.dot(left, right, preferred_element_type=jnp.float32)


def rows_product(left, right):
    return lax.dot_general(
        left, right, (((0,), (0,)), ((), ())), preferred_element_type=jnp.float32
    )


def against(left, right):
    return lax.dot_general(
        left, right, (((1,), (1,)), ((), ())), preferred_element_type=jnp.float32
    )


def body(tokens, gate_weights, up_weights, down_weights, rhs_gate, rhs_up, rhs_down, damping):
    dp, mp = lax.axis_size("dp"), lax.axis_size("mp")
    scale = 1.0 / (tokens.shape[0] * dp)
    rhs = (rhs_gate, rhs_up, rhs_down)
    axes = (0, 0, 1)

    def tangents(layer):
        return tuple(
            lax.all_gather(rhs[k][layer].astype(jnp.bfloat16), "dp", axis=axes[k], tiled=True)
            for k in range(3)
        )

    def scattered(grads):
        return tuple(
            lax.psum_scatter(
                grads[k].astype(jnp.bfloat16), "dp", scatter_dimension=axes[k], tiled=True
            ).astype(jnp.float32)
            for k in range(3)
        )

    whole = gathered(mp, tokens, 0)
    tangent_gate, tangent_up, tangent_down = tangents(0)
    next_gate, next_up, next_down = tangents(1)
    gate_one = matmul(whole, gate_weights[0])
    up_one = matmul(whole, up_weights[0])
    active_one, slope_one = silu_terms(gate_one)
    hidden_one = (active_one * up_one).astype(jnp.bfloat16)
    tan_gate = matmul(whole, tangent_gate)
    tan_up = matmul(whole, tangent_up)
    tan_hidden = (slope_one * up_one * tan_gate + active_one * tan_up).astype(jnp.bfloat16)
    layer_one, tan_layer = summed_whole(
        mp,
        (
            matmul(hidden_one, down_weights[0]),
            matmul(tan_hidden, down_weights[0]) + matmul(hidden_one, tangent_down),
        ),
        (whole, None),
        1,
    )
    gate_two = matmul(layer_one, gate_weights[1])
    up_two = matmul(layer_one, up_weights[1])
    active_two, slope_two = silu_terms(gate_two)
    hidden_two = (active_two * up_two).astype(jnp.bfloat16)
    tan_gate = matmul(tan_layer, gate_weights[1]) + matmul(layer_one, next_gate)
    tan_up = matmul(tan_layer, up_weights[1]) + matmul(layer_one, next_up)
    tan_hidden = (slope_two * up_two * tan_gate + active_two * tan_up).astype(jnp.bfloat16)
    (cotan,) = summed_whole(
        mp,
        (matmul(tan_hidden, down_weights[1]) + matmul(hidden_two, next_down),),
        (tan_layer,),
        2,
    )
    back_hidden = against(cotan, down_weights[1])
    back_gate = (back_hidden * up_two * slope_two).astype(jnp.bfloat16)
    back_up = (back_hidden * active_two).astype(jnp.bfloat16)
    (back_layer,) = summed_whole(
        mp,
        (against(back_gate, gate_weights[1]) + against(back_up, up_weights[1]),),
        (cotan,),
        3,
    )
    second = scattered(
        (
            rows_product(layer_one, back_gate),
            rows_product(layer_one, back_up),
            rows_product(hidden_two, cotan),
        )
    )
    back_hidden = against(back_layer, down_weights[0])
    back_gate = (back_hidden * up_one * slope_one).astype(jnp.bfloat16)
    back_up = (back_hidden * active_one).astype(jnp.bfloat16)
    first = scattered(
        (
            rows_product(whole, back_gate),
            rows_product(whole, back_up),
            rows_product(hidden_one, back_layer),
        )
    )
    grads = (first, second)
    norm = crossed = squared = 0.0
    for layer in range(2):
        for k in range(3):
            right, grad = rhs[k][layer], grads[layer][k]
            norm = norm + jnp.sum(right * right)
            crossed = crossed + jnp.sum(right * grad)
            squared = squared + jnp.sum(grad * grad)
    norm, crossed, squared = scalars_summed(dp, mp, (norm, crossed, squared), 4)
    damp = damping[0]
    along = crossed * scale + damp * norm
    image = squared * scale * scale + 2.0 * damp * scale * crossed + damp * damp * norm
    alpha = norm / along
    norm_next = norm - 2.0 * alpha * along + alpha * alpha * image
    beta = norm_next / norm
    steps = tuple(alpha * rhs[k] for k in range(3))
    nexts = tuple(
        jnp.stack(
            [
                rhs[k][layer]
                - alpha * (grads[layer][k] * scale + damp * rhs[k][layer])
                + beta * rhs[k][layer]
                for layer in range(2)
            ]
        )
        for k in range(3)
    )
    return steps + nexts


def solution(mesh):
    in_specs = (
        P("dp", "mp"),
        P(None, None, "mp"),
        P(None, None, "mp"),
        P(None, "mp", None),
        P(None, "dp", "mp"),
        P(None, "dp", "mp"),
        P(None, "mp", "dp"),
        P(),
    )
    out_specs = (
        P(None, "dp", "mp"),
        P(None, "dp", "mp"),
        P(None, "mp", "dp"),
        P(None, "dp", "mp"),
        P(None, "dp", "mp"),
        P(None, "mp", "dp"),
    )
    return jax.shard_map(body, mesh=mesh, in_specs=in_specs, out_specs=out_specs, check_vma=False)
```

time: 682 us -> 343 us (0.50)
  waiting for transfers between devices: 397 us -> 43.2 us
  blocking collectives: 153 us -> 0 us
  Pallas kernels: 0 us -> 149 us
  local copies, waits for them, and re-layouts: 6.29 us -> 21.6 us
  other arithmetic: 47.2 us -> 35 us
  matrix products: 52.5 us -> 61.3 us
  between operations: 24.7 us -> 31.6 us
    psum x2 -> x0, waiting for transfers between devices: 161 us -> none  [finish_first(): summed = lax.psum(partial_value, 'mp')]
    psum x2 -> x0, blocking collectives: 153 us -> none  [the longest x1 112 us: finish_first(): summed = lax.psum(partial_value, 'mp')]
    pallas_call x0 -> x5, Pallas kernels: none -> 149 us  [the longest x3 116 us: summed_whole(): pl.pallas_call(functools.partial(sum_kernel, outer, inner, count, which),...]
    all_gather x5 -> x6, waiting for transfers between devices: 135 us -> 0.03 us  [tangents(): lax.all_gather(rhs[k][layer].astype(jnp.bfloat16), 'dp', axis=axes[k], ti...]
    reduce_scatter x4 -> x6, waiting for transfers between devices: 100 us -> 41.4 us  [scattered(): lax.psum_scatter(grads[k].astype(jnp.bfloat16), 'dp', scatter_dimension=a...]
    convert_element_type x5 -> x0, other arithmetic: 14.2 us -> none  [the longest x1 3.56 us: curvature(): vectors[1].astype(jnp.bfloat16)]
    add x2 -> x0, other arithmetic: 13.3 us -> none  [body(): residual[k] + norm_next / norm_now * direction[k]]
    convert_element_type x0 -> x3, local copies, waits for them, and re-layouts: none -> 10.8 us  [tangents(): rhs[k][layer].astype(jnp.bfloat16)]
  transfers between devices with their start and end apart: 11 -> 12, of which waited for: 10 -> 4; matrix products, arithmetic and copies ran while one was open for 7% -> 21% of each run, Pallas kernels for 0% -> 31%
where the time goes in v1:
time: 343 us; the launch traced here: 342 us
  Pallas kernels  149 us (43%)
  matrix products  61.3 us (18%)
  waiting for transfers between devices  43.2 us (13%)
  other arithmetic  35 us (10%)
  between operations  31.6 us (9%)
  local copies, waits for them, and re-layouts  21.6 us (6%)
    pallas_call x3, Pallas kernels, summed_whole(): pl.pallas_call(functools.partial(sum_kernel, outer, inner, count, which),...  116 us
    reduce_scatter x6, waiting for transfers between devices, scattered(): lax.psum_scatter(grads[k].astype(jnp.bfloat16), 'dp', scatter_dimension=a...  41.4 us
    dot_general x13, matrix products, matmul(): return jnp.dot(left, right, preferred_element_type=jnp.float32)  39.6 us
    pallas_call x1, Pallas kernels, gathered(): pl.pallas_call(functools.partial(gather_kernel, outer, inner), out_shape=...  21.1 us
    another operation x5, other arithmetic, body(): jnp.stack([rhs[k][layer] - alpha * (grads[layer][k] * scale + damp * rhs[...  14.7 us
    dot_general x6, matrix products, rows_product(): lax.dot_general(left, right, (((0,), (0,)), ((), ())), preferred_element_...  12.5 us
    reduce_sum x3, other arithmetic, body(): norm = norm + jnp.sum(right * right)  12.3 us
    pallas_call x1, Pallas kernels, scalars_summed(): pl.pallas_call(functools.partial(scalar_kernel, dp, mp), out_shape=jax.Sh...  11.5 us
  transfers between devices with their start and end apart: 12, of which 4 were waited for; matrix products, arithmetic and copies ran while one was open for 21% of the time, Pallas kernels for 31%

profile of v1, /device:TPU:0, one launch (start us, length us, event | category | flops | bytes accessed | tf_op | source)
XLA Modules:
  0.0 342.2 jit_solution(15750325631844901791)
XLA Ops:
  7.2 3.6 %bitcast_convert_fusion.2 = (bf16[1024,448]{0,1:T(8,128)(2,1)}, bf16[1024,448]{0,1:T(8,128)(2,1)}) fusion(f32[2,1024,448]{1,2,0:T(8,128)} %param.12), kind=kLoop, calls=%fused_computation.114 | loop fusion | bytes 3670016 | tf_op jit(solution)/shard_map/convert_element_type | solution.py:264
  10.9 3.6 %bitcast_convert_fusion.1 = (bf16[1024,448]{0,1:T(8,128)(2,1)}, bf16[1024,448]{0,1:T(8,128)(2,1)}) fusion(f32[2,1024,448]{1,2,0:T(8,128)} %param.13), kind=kLoop, calls=%fused_computation.109 | loop fusion | bytes 3670016 | tf_op jit(solution)/shard_map/convert_element_type | solution.py:264
  14.5 3.7 %bitcast_convert_fusion = (bf16[448,1024]{1,0:T(8,128)(2,1)}, bf16[448,1024]{1,0:T(8,128)(2,1)}) fusion(f32[2,448,1024]{2,1,0:T(8,128)} %param.14), kind=kLoop, calls=%fused_computation.104 | loop fusion | bytes 3670016 | tf_op jit(solution)/shard_map/convert_element_type | solution.py:264
  20.0 21.1 %shard_map.127 = bf16[4,4,256,128]{3,2,1,0:T(8,128)(2,1)} custom-call(bf16[256,128]{1,0:T(8,128)(2,1)} %mine.1), custom_call_target="tpu_custom_call" | custom-call | bytes 16777216 | tf_op jit(solution)/shard_map/pallas_call | solution.py:182
  54.0 4.6 %fusion.64 = f32[256,2048]{1,0:T(8,128)S(1)} fusion(bf16[2,448,2048]{2,1,0:T(8,128)(2,1)} %param.11, f32[256,448]{0,1:T(8,128)} %convolution_multiply_fusion.1, bf16[2048,448]{0,1:T(8,128)(2,1)} %all-gather.9.cloned.1.call-done, bf16[32,8,16,128]{3,2,1,0:T(8,128)(2,1)S(1)} %bitcast.232, f32[256,448]{0,1:T(8,128)} %copy-done.16), kind=kOutput, calls=%fused_computation.95 | convolution fusion | flops 940326912 | bytes 7733248 | tf_op jit(solution)/shard_map/dot_general | solution.py:241
  58.6 3.2 fusion.2
  61.8 53.9 %shard_map.128 = (bf16[4,4,16,2048]{3,2,1,0:T(8,128)(2,1)}, bf16[4,4,16,2048]{3,2,1,0:T(8,128)(2,1)}) custom-call(bf16[4,4,16,2048]{3,2,1,0:T(8,128)(2,1)} %bitcast.238, bf16[4,4,16,2048]{3,2,1,0:T(8,128)(2,1)} %bitcast.225, bf16[4,4,16,2048]{3,2,1,0:T(8,128)(2,1)} %reshape_reshape.3.refs_2_), custom_call_target="tpu_custom_call" | custom-call | bytes 67108864 | tf_op jit(solution)/shard_map/pallas_call | solution.py:131
  115.8 3.3 fusion.60
  125.1 3.2 multiply_convert_fusion.4
  129.7 6.2 %fusion.49 = f32[256,2048]{1,0:T(8,128)} fusion(bf16[2,448,2048]{2,1,0:T(8,128)(2,1)} %param.11, f32[256,448]{0,1:T(8,128)} %fusion.102, f32[256,448]{0,1:T(8,128)} %fusion.132, bf16[256,2048]{1,0:T(8,128)(2,1)S(1)} %bitcast.237, bf16[2,2048,448]{1,2,0:T(8,128)(2,1)} %param.9, f32[256,448]{0,1:T(8,128)} %get-tuple-element.50, f32[256,448]{0,1:T(8,128)} %fusion.60), kind=kOutput, calls=%fused_computation.80 | convolution fusion | flops 940900352 | bytes 8650752 | tf_op jit(solution)/shard_map/dot_general | solution.py:241
  135.9 3.9 %fusion.3 = bf16[256,2048]{1,0:T(8,128)(2,1)} fusion(f32[256,2048]{1,0:T(8,128)} %fusion.49, bf16[256,448]{0,1:T(8,128)(2,1)} %get-tuple-element.49, bf16[448,2048]{1,0:T(8,128)(2,1)} %all-gather.17.cloned.1.call-done), kind=kOutput, calls=%fused_computation.34 | convolution fusion | flops 470810624 | bytes 5210112 | tf_op jit(solution)/shard_map/dot_general | solution.py:241
  139.8 32.4 %shard_map.129.refs_1_ = bf16[4,4,16,2048]{3,2,1,0:T(8,128)(2,1)} custom-call(bf16[4,4,16,2048]{3,2,1,0:T(8,128)(2,1)} %bitcast.226, bf16[4,4,16,2048]{3,2,1,0:T(8,128)(2,1)} %get-tuple-element.9.refs_1_), custom_call_target="tpu_custom_call" | custom-call | bytes 33554432 | tf_op jit(solution)/shard_map/pallas_call | solution.py:131
  181.2 29.8 %shard_map.130 = bf16[4,4,16,2048]{3,2,1,0:T(8,128)(2,1)} custom-call(bf16[4,4,16,2048]{3,2,1,0:T(8,128)(2,1)} %bitcast.227, bf16[4,4,16,2048]{3,2,1,0:T(8,128)(2,1)} %shard_map.129.refs_1_), custom_call_target="tpu_custom_call" | custom-call | bytes 33554432 | tf_op jit(solution)/shard_map/pallas_call | solution.py:131
  227.4 4.1 %fusion.73 = (f32[]{:T(128)}, f32[]{:T(128)}, f32[]{:T(128)}, f32[]{:T(128)}, f32[]{:T(128)}, /*index=5*/f32[]{:T(128)}) fusion(f32[2,1024,448]{1,2,0:T(8,128)} %param.12, bf16[1024,448]{0,1:T(8,128)(2,1)} %reduce-scatter.7.cloned.1.call-done, bf16[1024,448]{0,1:T(8,128)(2,1)} %reduce-scatter.13.cloned.1.call-done), kind=kLoop, calls=%fused_computation.116 | loop fusion | flops 6422522 | bytes 5505048 | tf_op jit(solution)/shard_map/reduce_sum | solution.py:339
  231.5 6.8 %reduce-scatter.15.cloned.1.call-done = bf16[1024,448]{0,1:T(8,128)(2,1)} async-done(((bf16[2048,448]{0,1:T(8,128)(2,1)}), bf16[1024,448]{0,1:T(8,128)(2,1)}) %reduce-scatter.15.cloned.1.call-update) | async-done | bytes 917520 | tf_op jit(solution)/shard_map/reduce_scatter | solution.py:270
  238.3 13.3 %reduce-scatter.9.cloned.1.call-done = bf16[1024,448]{0,1:T(8,128)(2,1)} async-done(((bf16[2048,448]{0,1:T(8,128)(2,1)}), bf16[1024,448]{0,1:T(8,128)(2,1)}) %reduce-scatter.9.cloned.1.call-update) | async-done | bytes 917520 | tf_op jit(solution)/shard_map/reduce_scatter | solution.py:270
  251.6 4.1 %fusion.72 = (f32[]{:T(128)}, f32[]{:T(128)}, f32[]{:T(128)}, f32[]{:T(128)}, f32[]{:T(128)}, /*index=5*/f32[]{:T(128)}) fusion(f32[2,1024,448]{1,2,0:T(8,128)} %param.13, bf16[1024,448]{0,1:T(8,128)(2,1)} %reduce-scatter.9.cloned.1.call-done, bf16[1024,448]{0,1:T(8,128)(2,1)} %reduce-scatter.15.cloned.1.call-done), kind=kLoop, calls=%fused_computation.111 | loop fusion | flops 6422522 | bytes 5505048 | tf_op jit(solution)/shard_map/reduce_sum | solution.py:339
  256.9 8.1 %reduce-scatter.17.cloned.1.call-done = bf16[448,1024]{1,0:T(8,128)(2,1)} async-done(((bf16[448,2048]{1,0:T(8,128)(2,1)}), bf16[448,1024]{1,0:T(8,128)(2,1)}) %reduce-scatter.17.cloned.1.call-update) | async-done | bytes 917520 | tf_op jit(solution)/shard_map/reduce_scatter | solution.py:270
  265.0 13.3 %reduce-scatter.11.cloned.1.call-done = bf16[448,1024]{1,0:T(8,128)(2,1)} async-done(((bf16[448,2048]{1,0:T(8,128)(2,1)}), bf16[448,1024]{1,0:T(8,128)(2,1)}) %reduce-scatter.11.cloned.1.call-update) | async-done | bytes 917520 | tf_op jit(solution)/shard_map/reduce_scatter | solution.py:270
  278.2 4.1 %fusion.71 = (f32[]{:T(128)}, f32[]{:T(128)}, f32[]{:T(128)}, f32[]{:T(128)}, f32[]{:T(128)}, /*index=5*/f32[]{:T(128)}) fusion(f32[2,448,1024]{2,1,0:T(8,128)} %param.14, bf16[448,1024]{1,0:T(8,128)(2,1)} %reduce-scatter.11.cloned.1.call-done, bf16[448,1024]{1,0:T(8,128)(2,1)} %reduce-scatter.17.cloned.1.call-done), kind=kLoop, calls=%fused_computation.106 | loop fusion | flops 6422522 | bytes 5505048 | tf_op jit(solution)/shard_map/reduce_sum | solution.py:339
  293.0 11.5 %shard_map.131 = f32[8,128]{1,0:T(8,128)} custom-call(f32[8,128]{1,0:T(8,128)} %broadcast_in_dim.2.mine), custom_call_target="tpu_custom_call" | custom-call | tf_op jit(solution)/shard_map/pallas_call | solution.py:224
  307.9 8.0 %broadcast_multiply_fusion.1 = (f32[2,1024,448]{1,2,0:T(8,128)}, f32[2,1024,448]{1,2,0:T(8,128)}) fusion(f32[2,1024,448]{1,2,0:T(8,128)} %param.13, f32[]{:T(128)S(6)} %div.14, f32[2,1024,448]{1,2,0:T(8,128)} %param.12), kind=kLoop, calls=%fused_computation.133 | loop fusion | flops 1835008 | bytes 14680068 | tf_op jit(solution)/shard_map/mul | solution.py:349
  319.2 4.4 %fusion.11 = (f32[1,1024,448]{1,2,0:T(8,128)S(1)}, f32[1,1024,448]{1,2,0:T(8,128)S(1)}, f32[1,1024,448]{1,2,0:T(8,128)S(1)}, f32[1,1024,448]{1,2,0:T(8,128)S(1)}) fusion(bf16[1024,448]{0,1:T(8,128)(2,1)S(1)} %copy-done.7, f32[2,1024,448]{1,2,0:T(8,128)} %param.12, f32[]{:T(128)S(6)} %div.15, f32[]{:T(128)} %bitcast.210, f32[]{:T(128)S(6)} %div.14, ...), kind=kLoop, calls=%fused_computation.42 | loop fusion | flops 14680064 | bytes 18350092 | tf_op jit(solution)/shard_map/stack | solution.py:351
  330.7 4.6 %pad_maximum_fusion.2 = (f32[2,448,1024]{2,1,0:T(8,128)}, f32[2,448,1024]{2,1,0:T(8,128)}) fusion(f32[1,448,1024]{2,1,0:T(8,128)S(1)} %get-tuple-element.29, f32[1,448,1024]{2,1,0:T(8,128)S(1)} %get-tuple-element.28, f32[2,448,1024]{2,1,0:T(8,128)S(1)} %copy-done, f32[]{:T(128)S(6)} %div.14), kind=kLoop, calls=%fused_computation.2 | loop fusion | flops 1835008 | bytes 14680068 | tf_op jit(solution)/shard_map/stack | solution.py:351
  (103 shorter events, 55.9 us)
Async XLA Ops:
  7.2 43.8 %all-gather.7.cloned.1.call-start = ((), (), s32[]{:S(2)}) async-start(), calls=%async_computation.6 | async-start | bytes 2752512 | tf_op jit(solution)/shard_map/all_gather | solution.py:264
  10.8 43.1 %all-gather.9.cloned.1.call-start = ((), (), s32[]{:S(2)}) async-start(), calls=%async_computation.7 | async-start | bytes 2752512 | tf_op jit(solution)/shard_map/all_gather | solution.py:264
  14.4 44.2 %all-gather.11.cloned.1.call-start = ((), (), s32[]{:S(2)}) async-start(), calls=%async_computation.8 | async-start | bytes 2752512 | tf_op jit(solution)/shard_map/all_gather | solution.py:264
  18.2 100.9 %all-gather.15.cloned.1.call-start = ((), (), s32[]{:S(2)}) async-start(), calls=%async_computation.10 | async-start | bytes 2752512 | tf_op jit(solution)/shard_map/all_gather | solution.py:264
  18.8 103.3 %all-gather.13.cloned.1.call-start = ((), (), s32[]{:S(2)}) async-start(), calls=%async_computation.9 | async-start | bytes 2752512 | tf_op jit(solution)/shard_map/all_gather | solution.py:264
  19.4 116.6 %all-gather.17.cloned.1.call-start = ((), (), s32[]{:S(2)}) async-start(), calls=%async_computation.11 | async-start | bytes 2752512 | tf_op jit(solution)/shard_map/all_gather | solution.py:264
  19.9 207.4 %reduce-scatter.13.cloned.1.call-start = ((), (), s32[]{:S(2)}) async-start(), calls=%async_computation.15 | async-start | bytes 2752512 | tf_op jit(solution)/shard_map/reduce_scatter | solution.py:270
  46.9 4.1 %copy-start.16 = (f32[256,448]{0,1:T(8,128)}, f32[256,448]{0,1:T(8,128)S(1)}, u32[]{:S(2)}) copy-start(f32[256,448]{0,1:T(8,128)S(1)} %fusion.69) | copy-start | bytes 1376260
  47.6 3.4 copy-start.18
  115.8 3.4 copy-start.1
  139.8 32.4 %copy-start.22 = (f32[256,448]{0,1:T(8,128)S(1)}, f32[256,448]{0,1:T(8,128)}, u32[]{:S(2)}) copy-start(f32[256,448]{0,1:T(8,128)} %fusion.60) | copy-start | bytes 1376260
  176.8 50.6 %reduce-scatter.7.cloned.1.call-start = ((), (), s32[]{:S(2)}) async-start(), calls=%async_computation.12 | async-start | bytes 2752512 | tf_op jit(solution)/shard_map/reduce_scatter | solution.py:270
  210.9 3.4 copy-start.17
  216.4 21.9 %reduce-scatter.15.cloned.1.call-start = ((), (), s32[]{:S(2)}) async-start(), calls=%async_computation.16 | async-start | bytes 2752512 | tf_op jit(solution)/shard_map/reduce_scatter | solution.py:270
  218.3 33.2 %reduce-scatter.9.cloned.1.call-start = ((), (), s32[]{:S(2)}) async-start(), calls=%async_computation.13 | async-start | bytes 2752512 | tf_op jit(solution)/shard_map/reduce_scatter | solution.py:270
  221.4 3.4 %copy-start.3 = (bf16[4,4,16,2048]{3,2,1,0:T(8,128)(2,1)S(1)}, bf16[4,4,16,2048]{3,2,1,0:T(8,128)(2,1)}, u32[]{:S(2)}) copy-start(bf16[4,4,16,2048]{3,2,1,0:T(8,128)(2,1)} %shard_map.130) | copy-start | bytes 3145732
  221.4 43.6 %reduce-scatter.17.cloned.1.call-start = ((), (), s32[]{:S(2)}) async-start(), calls=%async_computation.17 | async-start | bytes 2752512 | tf_op jit(solution)/shard_map/reduce_scatter | solution.py:270
  224.5 53.7 %reduce-scatter.11.cloned.1.call-start = ((), (), s32[]{:S(2)}) async-start(), calls=%async_computation.14 | async-start | bytes 2752512 | tf_op jit(solution)/shard_map/reduce_scatter | solution.py:270
  307.8 11.3 %copy-start.6 = (bf16[1024,448]{0,1:T(8,128)(2,1)S(1)}, bf16[1024,448]{0,1:T(8,128)(2,1)}, u32[]{:S(2)}) copy-start(bf16[1024,448]{0,1:T(8,128)(2,1)} %reduce-scatter.13.cloned.1.call-done) | copy-start | bytes 2752516
  307.8 11.3 %copy-start.7 = (bf16[1024,448]{0,1:T(8,128)(2,1)S(1)}, bf16[1024,448]{0,1:T(8,128)(2,1)}, u32[]{:S(2)}) copy-start(bf16[1024,448]{0,1:T(8,128)(2,1)} %reduce-scatter.7.cloned.1.call-done) | copy-start | bytes 2752516
  307.9 11.3 %copy-start.8 = (bf16[1024,448]{0,1:T(8,128)(2,1)S(1)}, bf16[1024,448]{0,1:T(8,128)(2,1)}, u32[]{:S(2)}) copy-start(bf16[1024,448]{0,1:T(8,128)(2,1)} %reduce-scatter.15.cloned.1.call-done) | copy-start | bytes 2752516
  325.9 3.4 copy-start
  325.9 3.6 %copy-start.4 = (bf16[448,1024]{1,0:T(8,128)(2,1)S(1)}, bf16[448,1024]{1,0:T(8,128)(2,1)}, u32[]{:S(2)}) copy-start(bf16[448,1024]{1,0:T(8,128)(2,1)} %reduce-scatter.17.cloned.1.call-done) | copy-start | bytes 2752516
  325.9 3.9 %copy-start.5 = (bf16[448,1024]{1,0:T(8,128)(2,1)S(1)}, bf16[448,1024]{1,0:T(8,128)(2,1)}, u32[]{:S(2)}) copy-start(bf16[448,1024]{1,0:T(8,128)(2,1)} %reduce-scatter.11.cloned.1.call-done) | copy-start | bytes 2752516
  (11 other events, 26.7 us)
Sparse Core Ops, SparseCore 0:
  10.9 12.9 all-gather.6
  26.0 11.3 all-gather.8
  39.0 11.3 all-gather.10
  52.3 11.3 all-gather.14
  65.7 11.3 all-gather.12
  78.5 11.3 all-gather.16
  176.9 8.7 reduce-scatter.12
  216.5 8.3 reduce-scatter.6
  227.7 10.5 reduce-scatter.14
  241.0 10.5 reduce-scatter.8
  254.4 10.5 reduce-scatter.16
  267.6 10.5 reduce-scatter.10

commit v2 on v1

v2 whole, which is shorter than its diff:
```python
import functools
import jax
import jax.numpy as jnp
from jax import lax
from jax.experimental import pallas as pl
from jax.experimental.pallas import tpu as pltpu
from jax.sharding import PartitionSpec as P

ITERS = 1
MESH = pl.DeviceIdType.MESH


def split_of(count):
    inner = 1
    while inner * inner < count and count % (inner * 2) == 0:
        inner *= 2
    return count // inner, inner


def greet(peers):
    barrier = pltpu.get_barrier_semaphore()
    for peer in peers:
        pl.semaphore_signal(barrier, inc=1, device_id=peer, device_id_type=MESH)
    pl.semaphore_wait(barrier, len(peers))


def place(outer, inner):
    me = lax.axis_index("mp")
    far, near = lax.div(me, inner), lax.rem(me, inner)

    def along_outer(step):
        return {"mp": lax.rem(far + step, outer) * inner + near}

    def along_inner(step):
        return {"mp": far * inner + lax.rem(near + step, inner)}

    return far, near, along_outer, along_inner


def remote(source, target, send, receive, peer):
    copy = pltpu.make_async_remote_copy(
        src_ref=source, dst_ref=target, send_sem=send, recv_sem=receive,
        device_id=peer, device_id_type=MESH,
    )
    copy.start()
    return copy


def start_pairs(sources, pairs, send, receive):
    row = lax.axis_index("dp")
    copies = []
    for k, (source, pair) in enumerate(zip(sources, pairs)):
        width = pair.shape[-1]
        if source.shape[-1] == width:
            outgoing = source
        else:
            outgoing = source.at[:, pl.ds(pl.multiple_of((1 - row) * width, width), width)]
        copies.append(remote(outgoing, pair.at[1], send.at[k], receive.at[k], {"dp": 1 - row}))
    return copies


def keep_pairs(sources, pairs):
    row = lax.axis_index("dp")
    for source, pair in zip(sources, pairs):
        width = pair.shape[-1]
        if source.shape[-1] == width:
            pair[0] = source[...]
        else:
            pair[0] = source[:, pl.ds(pl.multiple_of(row * width, width), width)]


def sum_kernel(outer, inner, count, adds, paired, *refs):
    parts = refs[:count]
    extra = dict(zip(adds, refs[count:count + len(adds)]))
    base = count + len(adds)
    sources = refs[base:base + paired]
    base += paired
    outs = refs[base:base + count]
    base += count
    pairs = refs[base:base + paired]
    base += paired
    near_slots, held, far_slots, s1s, s1r, s2s, s2r, g1s, g1r, g2s, g2r = refs[base:base + 11]
    far, near, along_outer, along_inner = place(outer, inner)
    peers = [along_outer(e) for e in range(1, outer)] + [along_inner(d) for d in range(1, inner)]
    if paired:
        peers.append({"dp": 1 - lax.axis_index("dp")})
    greet(peers)
    order = list(range(1, outer)) + [0]
    copies = []
    first, second, third, fourth = {}, {}, {}, {}
    for e in order:
        piece = lax.rem(far + e, outer)
        for k in range(count):
            for d in range(1, inner):
                first[k, d, e] = remote(
                    parts[k].at[lax.rem(near + d, inner), piece], near_slots.at[k, d, e],
                    s1s.at[k, d, e], s1r.at[k, d, e], along_inner(d),
                )
    swaps = start_pairs(sources, pairs, *refs[base + 11:]) if paired else []
    keep_pairs(sources, pairs)
    own = {}
    for e in order:
        piece = lax.rem(far + e, outer)
        for k in range(count):
            total = parts[k][near, piece].astype(jnp.float32)
            for d in range(1, inner):
                first[k, d, e].wait_recv()
                total = total + near_slots[k, d, e].astype(jnp.float32)
            if e:
                held[k, e] = total.astype(jnp.bfloat16)
                second[k, e] = remote(
                    held.at[k, e], far_slots.at[k, e], s2s.at[k, e], s2r.at[k, e], along_outer(e)
                )
            else:
                own[k] = total
    for k in range(count):
        total = own[k]
        for e in range(1, outer):
            second[k, e].wait_recv()
            total = total + far_slots[k, e].astype(jnp.float32)
        if k in extra:
            total = total + extra[k][near, far].astype(jnp.float32)
        outs[k][near, far] = total.astype(jnp.bfloat16)
        spread(outer, inner, outs[k], far, near, along_outer, along_inner, third, fourth, k,
               g1s, g1r, g2s, g2r)
    forward(outer, inner, outs, far, near, along_inner, third, fourth, g2s, g2r)
    for copy in swaps:
        copy.wait()
    for table in (first, second, third, fourth):
        for copy in table.values():
            copy.wait_send()


def spread(outer, inner, out, far, near, along_outer, along_inner, third, fourth, k, g1s, g1r, g2s, g2r):
    for e in range(1, outer):
        third[k, e] = remote(out.at[near, far], out.at[near, far], g1s.at[k, e], g1r.at[k, e], along_outer(e))
    for d in range(1, inner):
        fourth[k, d, 0] = remote(
            out.at[near, far], out.at[near, far], g2s.at[k, d, 0], g2r.at[k, d, 0], along_inner(d)
        )


def forward(outer, inner, outs, far, near, along_inner, third, fourth, g2s, g2r):
    for e in range(1, outer):
        piece = lax.rem(far - e + outer, outer)
        for k in range(len(outs)):
            third[k, e].wait_recv()
            for d in range(1, inner):
                fourth[k, d, e] = remote(
                    outs[k].at[near, piece], outs[k].at[near, piece],
                    g2s.at[k, d, e], g2r.at[k, d, e], along_inner(d),
                )
    for copy in fourth.values():
        copy.wait_recv()


def summed_whole(mp, parts, adds, ident, full=(), half=()):
    outer, inner = split_of(mp)
    rows, width = parts[0].shape
    share = rows // mp
    count = len(parts)
    view = (inner, outer, share, width)
    which = tuple(k for k in range(count) if adds[k] is not None)
    operands = [p.astype(jnp.bfloat16).reshape(view) for p in parts]
    operands += [adds[k].reshape(view) for k in which]
    dma = pltpu.SemaphoreType.DMA
    paired = len(full) + len(half)
    operands += list(full) + list(half)
    outs = pl.pallas_call(
        functools.partial(sum_kernel, outer, inner, count, which, paired),
        out_shape=[jax.ShapeDtypeStruct(view, jnp.bfloat16)] * count + pair_shapes(full, half),
        in_specs=[pl.BlockSpec(memory_space=pltpu.VMEM)] * len(operands),
        out_specs=[pl.BlockSpec(memory_space=pltpu.VMEM)] * (count + paired),
        scratch_shapes=[
            pltpu.VMEM((count, inner, outer, share, width), jnp.bfloat16),
            pltpu.VMEM((count, outer, share, width), jnp.bfloat16),
            pltpu.VMEM((count, outer, share, width), jnp.bfloat16),
            dma((count, inner, outer)), dma((count, inner, outer)),
            dma((count, outer)), dma((count, outer)),
            dma((count, outer)), dma((count, outer)),
            dma((count, inner, outer)), dma((count, inner, outer)),
        ] + [dma((paired,))] * (2 if paired else 0),
        cost_estimate=pl.CostEstimate(
            flops=0, bytes_accessed=count * rows * width * 64, transcendentals=0
        ),
        compiler_params=pltpu.CompilerParams(collective_id=ident, has_side_effects=True),
    )(*operands)
    return [o.reshape(rows, width) for o in outs[:count]] + joined(outs[count:])


def pair_shapes(full, half):
    return [jax.ShapeDtypeStruct((2,) + x.shape, x.dtype) for x in full] + [
        jax.ShapeDtypeStruct((2, x.shape[0], x.shape[1] // 2), x.dtype) for x in half
    ]


def joined(pairs):
    return [p.reshape(2 * p.shape[1], p.shape[2]) for p in pairs]


def pair_kernel(paired, *refs):
    sources, pairs = refs[:paired], refs[paired:2 * paired]
    greet([{"dp": 1 - lax.axis_index("dp")}])
    copies = start_pairs(sources, pairs, *refs[2 * paired:])
    keep_pairs(sources, pairs)
    for copy in copies:
        copy.wait()


def swapped(full, half, ident):
    paired = len(full) + len(half)
    spec = [pl.BlockSpec(memory_space=pltpu.VMEM)] * paired
    dma = pltpu.SemaphoreType.DMA
    return joined(
        pl.pallas_call(
            functools.partial(pair_kernel, paired),
            out_shape=pair_shapes(full, half),
            in_specs=spec,
            out_specs=spec,
            scratch_shapes=[dma((paired,)), dma((paired,))],
            compiler_params=pltpu.CompilerParams(collective_id=ident, has_side_effects=True),
        )(*full, *half)
    )


def chunk_of(rows):
    return next(c for c in (64, 112, 32, 16, 8) if rows % c == 0)


def folded(block):
    return jnp.sum(block.reshape(block.shape[0] // 8, 8, block.shape[1]), axis=0)


def gather_kernel(outer, inner, mine, gate, up, down, out, norm, *refs):
    tangents, scratch = refs[:6], refs[6:]
    held, local, loads, g1s, g1r, g2s, g2r, ts, tr = scratch
    blocks = [(source, layer) for layer in range(2) for source in (gate, up, down)]
    fetches = []
    for k, (source, layer) in enumerate(blocks):
        fetches.append(pltpu.make_async_copy(source.at[layer], held.at[k], loads.at[k]))
        fetches[k].start()
    far, near, along_outer, along_inner = place(outer, inner)
    row = lax.axis_index("dp")
    greet(
        [along_outer(e) for e in range(1, outer)]
        + [along_inner(d) for d in range(1, inner)]
        + [{"dp": 1 - row}]
    )
    third, fourth = {}, {}
    keep = pltpu.make_async_copy(mine, out.at[far, near], local)
    keep.start()
    for e in range(1, outer):
        third[e] = remote(mine, out.at[far, near], g1s.at[e], g1r.at[e], along_outer(e))
    for d in range(1, inner):
        fourth[d, 0] = remote(mine, out.at[far, near], g2s.at[d, 0], g2r.at[d, 0], along_inner(d))
    rows, width = held.shape[1:]
    chunk = chunk_of(rows)
    columns = pl.ds(pl.multiple_of(row * width, width), width)
    total = jnp.zeros((8, width), jnp.float32)
    swaps = []

    def convert(k, total):
        fetches[k].wait()

        def piece(step, carry):
            span = pl.ds(pl.multiple_of(step * chunk, chunk), chunk)
            value = held[k, span]
            tangents[k][span, columns] = value.astype(jnp.bfloat16)
            return carry + folded(value * value)

        total = lax.fori_loop(0, rows // chunk, piece, total)
        swaps.append(
            remote(tangents[k].at[:, columns], tangents[k].at[:, columns], ts.at[k], tr.at[k], {"dp": 1 - row})
        )
        return total

    def relay(e):
        piece = lax.rem(far - e + outer, outer)
        third[e].wait_recv()
        for d in range(1, inner):
            fourth[d, e] = remote(
                out.at[piece, near], out.at[piece, near], g2s.at[d, e], g2r.at[d, e], along_inner(d)
            )

    total = convert(0, total)
    total = convert(1, total)
    for e in range(1, outer):
        relay(e)
    for k in range(2, 6):
        total = convert(k, total)
    norm[...] = total
    for copy in fourth.values():
        copy.wait_recv()
    keep.wait()
    for copy in swaps:
        copy.wait()
    for table in (third, fourth):
        for copy in table.values():
            copy.wait_send()


def gathered(mp, tokens, rhs, ident):
    outer, inner = split_of(mp)
    rows, share = tokens.shape
    hidden, width = rhs[0].shape[1:]
    dma = pltpu.SemaphoreType.DMA
    vmem, anywhere = pl.BlockSpec(memory_space=pltpu.VMEM), pl.BlockSpec(memory_space=pl.ANY)
    out, norm, *tangents = pl.pallas_call(
        functools.partial(gather_kernel, outer, inner),
        out_shape=[
            jax.ShapeDtypeStruct((outer, inner, rows, share), tokens.dtype),
            jax.ShapeDtypeStruct((8, width), jnp.float32),
        ] + [jax.ShapeDtypeStruct((hidden, 2 * width), jnp.bfloat16)] * 6,
        in_specs=[vmem] + [anywhere] * 3,
        out_specs=[vmem] * 8,
        scratch_shapes=[
            pltpu.VMEM((6, hidden, width), jnp.float32),
            dma, dma((6,)), dma((outer,)), dma((outer,)), dma((inner, outer)), dma((inner, outer)),
            dma((6,)), dma((6,)),
        ],
        compiler_params=pltpu.CompilerParams(
            collective_id=ident, has_side_effects=True, vmem_limit_bytes=48 * 1024 * 1024
        ),
    )(tokens, *rhs)
    whole = out.reshape(mp, rows, share).transpose(1, 0, 2).reshape(rows, mp * share)
    return whole, norm, tangents


def scalar_kernel(dp, mp, scale, norm, damping, gate, up, down, *refs):
    grads, (out, right, held, packed, slots, loads, send, receive) = refs[:6], refs[6:]
    row, column = lax.axis_index("dp"), lax.axis_index("mp")
    total = dp * mp
    me = row * mp + column

    def other(step):
        index = lax.rem(me + step, total)
        return {"dp": lax.div(index, mp), "mp": lax.rem(index, mp)}

    barrier = pltpu.get_barrier_semaphore()
    for step in range(1, total):
        pl.semaphore_signal(barrier, inc=1, device_id=other(step), device_id_type=MESH)
    blocks = [(source, layer) for layer in range(2) for source in (gate, up, down)]
    fetches = []
    for k, (source, layer) in enumerate(blocks):
        fetches.append(
            (
                pltpu.make_async_copy(source.at[layer], right.at[k], loads.at[k, 0]),
                pltpu.make_async_copy(grads[k], held.at[k], loads.at[k, 1]),
            )
        )
        for fetch in fetches[k]:
            fetch.start()
    rows, width = right.shape[1:]
    chunk = chunk_of(rows)
    zero = jnp.zeros((8, width), jnp.float32)
    sums = (zero, zero)
    for k in range(6):
        for fetch in fetches[k]:
            fetch.wait()

        def piece(step, carry):
            span = pl.ds(pl.multiple_of(step * chunk, chunk), chunk)
            value, grad = right[k, span], held[k, span]
            return carry[0] + folded(value * grad), carry[1] + folded(grad * grad)

        sums = lax.fori_loop(0, rows // chunk, piece, sums)
    for k, value in enumerate((norm[...],) + sums):
        narrow = value[:, :128]
        for lane in range(128, width, 128):
            narrow = narrow + value[:, lane:lane + 128]
        packed[k] = narrow
    pl.semaphore_wait(barrier, total - 1)
    copies = [
        remote(packed, slots.at[me], send.at[step], receive.at[step], other(step))
        for step in range(1, total)
    ]
    slots[me] = packed[...]
    for copy in copies:
        copy.wait_recv()
    whole = jnp.sum(slots[...], axis=0)
    normed, crossed, squared = (jnp.sum(whole[k], axis=(0, 1), keepdims=True) for k in range(3))
    damp = damping[...]
    along = crossed * scale + damp * normed
    image = squared * (scale * scale) + 2.0 * damp * scale * crossed + damp * damp * normed
    alpha = normed / along
    after = normed - 2.0 * alpha * along + alpha * alpha * image
    beta = after / normed
    for k, value in enumerate((alpha, 1.0 + beta - alpha * damp, alpha * scale)):
        out[k:k + 1] = jnp.broadcast_to(value, (1, 128))
    for copy in copies:
        copy.wait_send()


def coefficients(dp, mp, scale, norm, damping, rhs, grads, ident):
    total = dp * mp
    hidden, width = rhs[0].shape[1:]
    dma = pltpu.SemaphoreType.DMA
    vmem, anywhere = pl.BlockSpec(memory_space=pltpu.VMEM), pl.BlockSpec(memory_space=pl.ANY)
    out = pl.pallas_call(
        functools.partial(scalar_kernel, dp, mp, scale),
        out_shape=jax.ShapeDtypeStruct((8, 128), jnp.float32),
        in_specs=[vmem, vmem] + [anywhere] * 9,
        out_specs=vmem,
        scratch_shapes=[
            pltpu.VMEM((6, hidden, width), jnp.float32),
            pltpu.VMEM((6, hidden, width), jnp.float32),
            pltpu.VMEM((3, 8, 128), jnp.float32),
            pltpu.VMEM((total, 3, 8, 128), jnp.float32),
            dma((6, 2)), dma((total,)), dma((total,)),
        ],
        compiler_params=pltpu.CompilerParams(
            collective_id=ident, has_side_effects=True, vmem_limit_bytes=32 * 1024 * 1024
        ),
    )(norm, damping.reshape(1, 1), *rhs, *grads)
    return out[0, 0], out[1, 0], out[2, 0]


def silu_terms(value):
    sigmoid_value = jax.nn.sigmoid(value)
    return (value * sigmoid_value, sigmoid_value * (1.0 + value * (1.0 - sigmoid_value)))


def matmul(left, right):
    return jnp.dot(left, right, preferred_element_type=jnp.float32)


def rows_product(left, right):
    return lax.dot_general(
        left, right, (((0,), (0,)), ((), ())), preferred_element_type=jnp.float32
    )


def against(left, right):
    return lax.dot_general(
        left, right, (((1,), (1,)), ((), ())), preferred_element_type=jnp.float32
    )


def body(tokens, gate_weights, up_weights, down_weights, rhs_gate, rhs_up, rhs_down, damping):
    dp, mp = lax.axis_size("dp"), lax.axis_size("mp")
    scale = 1.0 / (tokens.shape[0] * dp)
    turned = (rhs_gate.transpose(0, 2, 1), rhs_up.transpose(0, 2, 1), rhs_down)
    whole, norm, tangents = gathered(mp, tokens, turned, 0)
    tangent_gate, tangent_up, tangent_down, later_gate, later_up, later_down = tangents
    gate_one = matmul(whole, gate_weights[0])
    up_one = matmul(whole, up_weights[0])
    active_one, slope_one = silu_terms(gate_one)
    hidden_one = (active_one * up_one).astype(jnp.bfloat16)
    tan_gate = against(whole, tangent_gate)
    tan_up = against(whole, tangent_up)
    tan_hidden = (slope_one * up_one * tan_gate + active_one * tan_up).astype(jnp.bfloat16)
    layer_one, tan_layer = summed_whole(
        mp,
        (
            matmul(hidden_one, down_weights[0]),
            matmul(tan_hidden, down_weights[0]) + matmul(hidden_one, tangent_down),
        ),
        (whole, None),
        1,
    )
    gate_two = matmul(layer_one, gate_weights[1])
    up_two = matmul(layer_one, up_weights[1])
    active_two, slope_two = silu_terms(gate_two)
    hidden_two = (active_two * up_two).astype(jnp.bfloat16)
    tan_gate = matmul(tan_layer, gate_weights[1]) + against(layer_one, later_gate)
    tan_up = matmul(tan_layer, up_weights[1]) + against(layer_one, later_up)
    tan_hidden = (slope_two * up_two * tan_gate + active_two * tan_up).astype(jnp.bfloat16)
    (cotan,) = summed_whole(
        mp,
        (matmul(tan_hidden, down_weights[1]) + matmul(hidden_two, later_down),),
        (tan_layer,),
        2,
    )
    back_hidden = against(cotan, down_weights[1])
    back_gate = (back_hidden * up_two * slope_two).astype(jnp.bfloat16)
    back_up = (back_hidden * active_two).astype(jnp.bfloat16)
    back_layer, gates, ups, hiddens, first_hiddens, layers, cotans, inputs = summed_whole(
        mp,
        (against(back_gate, gate_weights[1]) + against(back_up, up_weights[1]),),
        (cotan,),
        3,
        (back_gate, back_up, hidden_two, hidden_one),
        (layer_one, cotan, whole),
    )
    second = (rows_product(gates, layers), rows_product(ups, layers), rows_product(hiddens, cotans))
    back_hidden = against(back_layer, down_weights[0])
    back_gate = (back_hidden * up_one * slope_one).astype(jnp.bfloat16)
    back_up = (back_hidden * active_one).astype(jnp.bfloat16)
    gates, ups, backs = swapped((back_gate, back_up), (back_layer,), 5)
    first = (rows_product(gates, inputs), rows_product(ups, inputs), rows_product(first_hiddens, backs))
    grads = (first, second)
    alpha, keep, drop = coefficients(dp, mp, scale, norm, damping, turned, first + second, 4)
    steps = [alpha * turned[k] for k in range(3)]
    nexts = [
        jnp.stack([keep * turned[k][layer] - drop * grads[layer][k] for layer in range(2)])
        for k in range(3)
    ]
    for arrays in (steps, nexts):
        arrays[0], arrays[1] = arrays[0].transpose(0, 2, 1), arrays[1].transpose(0, 2, 1)
    return tuple(steps) + tuple(nexts)


def solution(mesh):
    in_specs = (
        P("dp", "mp"),
        P(None, None, "mp"),
        P(None, None, "mp"),
        P(None, "mp", None),
        P(None, "dp", "mp"),
        P(None, "dp", "mp"),
        P(None, "mp", "dp"),
        P(),
    )
    out_specs = (
        P(None, "dp", "mp"),
        P(None, "dp", "mp"),
        P(None, "mp", "dp"),
        P(None, "dp", "mp"),
        P(None, "dp", "mp"),
        P(None, "mp", "dp"),
    )
    return jax.shard_map(body, mesh=mesh, in_specs=in_specs, out_specs=out_specs, check_vma=False)
```

time: 343 us -> 257 us (0.75)
  waiting for transfers between devices: 43.2 us -> 0 us
  between operations: 31.6 us -> 1.79 us
  Pallas kernels: 149 us -> 167 us
  matrix products: 61.3 us -> 44.5 us
  other arithmetic: 35 us -> 27.4 us
  local copies, waits for them, and re-layouts: 21.6 us -> 15.6 us
    reduce_scatter x6 -> x0, waiting for transfers between devices: 41.4 us -> none  [scattered(): lax.psum_scatter(grads[k].astype(jnp.bfloat16), 'dp', scatter_dimension=a...]
    pallas_call x4 -> x5, Pallas kernels: 128 us -> 145 us  [the longest x3 124 us: summed_whole(): pl.pallas_call(functools.partial(sum_kernel, outer, inner, count, which,...]
    dot_general x13 -> x10, matrix products: 39.6 us -> 24.8 us  [matmul(): return jnp.dot(left, right, preferred_element_type=jnp.float32)]
    reduce_sum x3 -> x0, other arithmetic: 12.3 us -> none  [body(): norm = norm + jnp.sum(right * right)]
    convert_element_type x3 -> x0, local copies, waits for them, and re-layouts: 10.8 us -> none  [tangents(): rhs[k][layer].astype(jnp.bfloat16)]
    unnamed x46 -> x91, local copies, waits for them, and re-layouts: 5.61 us -> 13 us
    dot_general x6, matrix products: 12.5 us -> 5.29 us  [rows_product(): lax.dot_general(left, right, (((0,), (0,)), ((), ())), preferred_element_...]
    dot_general x4 -> x7, matrix products: 9.27 us -> 14.5 us  [against(): lax.dot_general(left, right, (((1,), (1,)), ((), ())), preferred_element_...]
  transfers between devices with their start and end apart: 12 -> 0, of which waited for: 4 -> 0; matrix products, arithmetic and copies ran while one was open for 21% -> 0% of each run, Pallas kernels for 31% -> 0%
where the time goes in v2:
time: 257 us
  Pallas kernels  167 us (65%)
  matrix products  44.5 us (17%)
  other arithmetic  27.4 us (11%)
  local copies, waits for them, and re-layouts  15.6 us (6%)
    pallas_call x3, Pallas kernels, summed_whole(): pl.pallas_call(functools.partial(sum_kernel, outer, inner, count, which,...  124 us
    dot_general x10, matrix products, matmul(): return jnp.dot(left, right, preferred_element_type=jnp.float32)  24.8 us
    pallas_call x1, Pallas kernels, gathered(): pl.pallas_call(functools.partial(gather_kernel, outer, inner), out_shape=...  22.5 us
    another operation x3, other arithmetic, body(): jnp.stack([keep * turned[k][layer] - drop * grads[layer][k] for layer in...  18.2 us
    pallas_call x1, Pallas kernels, coefficients(): pl.pallas_call(functools.partial(scalar_kernel, dp, mp, scale), out_shape...  15.4 us
    dot_general x7, matrix products, against(): lax.dot_general(left, right, (((1,), (1,)), ((), ())), preferred_element_...  14.5 us
    unnamed x91, local copies, waits for them, and re-layouts  13 us
    pallas_call x1, Pallas kernels, swapped(): pl.pallas_call(functools.partial(pair_kernel, paired), out_shape=pair_sha...  5.51 us

profile of v2, /device:TPU:0, one launch (start us, length us, event | category | flops | bytes accessed | tf_op | source)
XLA Modules:
  0.0 256.7 jit_solution(6036953178558366554)
XLA Ops:
  2.1 22.5 %shard_map.127 = (bf16[4,4,256,128]{3,2,1,0:T(8,128)(2,1)S(1)}, f32[8,1024]{1,0:T(8,128)S(1)}, bf16[448,2048]{1,0:T(8,128)(2,1)S(1)}, bf16[448,2048]{1,0:T(8,128...) custom-call(bf16[256,128]{1,0:T(8,128)(2,1)S(1)} %copy-done.9, ...), custom_call_target="tpu_custom_call" | custom-call | tf_op jit(solution)/shard_map/pallas_call | solution.py:308
  28.9 1.6 convolution_multiply_fusion.1
  30.5 4.6 %fusion.34 = f32[256,2048]{1,0:T(8,128)} fusion(bf16[2,448,2048]{2,1,0:T(8,128)(2,1)} %param.11, f32[256,448]{1,0:T(8,128)} %convolution_multiply_fusion.1, bf16[448,2048]{1,0:T(8,128)(2,1)S(1)} %get-tuple-element.30, f32[256,448]{1,0:T(8,128)} %copy-done.40, bf16[32,8,16,128]{3,2,1,0:T(8,128)(2,1)S(1)} %bitcast.185), kind=kOutput, calls=%fused_computation.47 | convolution fusion | flops 940326912 | bytes 7864320 | tf_op jit(solution)/shard_map/dot_general | solution.py:424
  35.0 4.0 %fusion = bf16[256,2048]{1,0:T(8,128)(2,1)} fusion(f32[256,2048]{1,0:T(8,128)} %fusion.34, bf16[256,448]{1,0:T(8,128)(2,1)S(1)} %get-tuple-element.63.refs_5_, bf16[448,2048]{1,0:T(8,128)(2,1)} %get-tuple-element.31), kind=kOutput, calls=%fused_computation.7 | convolution fusion | flops 470810624 | bytes 5210112 | tf_op jit(solution)/shard_map/dot_general | solution.py:424
  39.0 1.7 convolution_convert_fusion
  42.0 55.8 %shard_map.128 = (bf16[4,4,16,2048]{3,2,1,0:T(8,128)(2,1)}, bf16[4,4,16,2048]{3,2,1,0:T(8,128)(2,1)}) custom-call(bf16[4,4,16,2048]{3,2,1,0:T(8,128)(2,1)} %bitcast.196, bf16[4,4,16,2048]{3,2,1,0:T(8,128)(2,1)} %bitcast.190, bf16[4,4,16,2048]{3,2,1,0:T(8,128)(2,1)} %reshape_reshape.3.refs_2_), custom_call_target="tpu_custom_call" | custom-call | bytes 67108864 | tf_op jit(solution)/shard_map/pallas_call | solution.py:169
  97.9 2.7 %fusion.82 = f32[256,448]{1,0:T(8,128)S(1)} fusion(bf16[256,2048]{1,0:T(8,128)(2,1)} %bitcast.199, bf16[448,2048]{1,0:T(8,128)(2,1)} %get-tuple-element.35), kind=kOutput, calls=%fused_computation.103 | convolution fusion | flops 469762048 | bytes 3342336 | tf_op jit(solution)/shard_map/dot_general | solution.py:434
  106.6 5.9 %fusion.19 = f32[256,2048]{1,0:T(8,128)} fusion(bf16[2,448,2048]{2,1,0:T(8,128)(2,1)} %param.11, f32[256,448]{1,0:T(8,128)} %fusion.66, f32[256,448]{1,0:T(8,128)} %fusion.81, bf16[256,2048]{1,0:T(8,128)(2,1)} %bitcast.194, bf16[2,2048,448]{1,2,0:T(8,128)(2,1)} %param.9, f32[256,448]{1,0:T(8,128)} %get-tuple-element.66, f32[256,448]{1,0:T(8,128)} %copy-done.38), kind=kOutput, calls=%fused_computation.32 | convolution fusion | flops 940900352 | bytes 8912896 | tf_op jit(solution)/shard_map/dot_general | solution.py:424
  112.6 3.3 %fusion.1 = bf16[256,2048]{1,0:T(8,128)(2,1)} fusion(f32[256,2048]{1,0:T(8,128)} %fusion.19, bf16[256,448]{1,0:T(8,128)(2,1)S(1)} %get-tuple-element.65.refs_4_, bf16[448,2048]{1,0:T(8,128)(2,1)S(1)} %copy-done.16), kind=kOutput, calls=%fused_computation.8 | convolution fusion | flops 470810624 | bytes 5210112 | tf_op jit(solution)/shard_map/dot_general | solution.py:424
  115.9 33.1 %shard_map.129.refs_1_ = bf16[4,4,16,2048]{3,2,1,0:T(8,128)(2,1)} custom-call(bf16[4,4,16,2048]{3,2,1,0:T(8,128)(2,1)} %bitcast.191, bf16[4,4,16,2048]{3,2,1,0:T(8,128)(2,1)} %get-tuple-element.33.refs_1_), custom_call_target="tpu_custom_call" | custom-call | bytes 33554432 | tf_op jit(solution)/shard_map/pallas_call | solution.py:169
  149.0 2.8 %multiply_convert_fusion.2 = (bf16[256,448]{1,0:T(8,128)(2,1)S(1)}, bf16[256,448]{1,0:T(8,128)(2,1)S(1)}) fusion(f32[256,448]{1,0:T(8,128)S(1)} %copy-done.39, f32[256,448]{1,0:T(8,128)S(1)} %copy-done.42, bf16[256,2048]{1,0:T(8,128)(2,1)} %bitcast.188, bf16[2,448,2048]{2,1,0:T(8,128)(2,1)} %param.11), kind=kOutput, calls=%fused_computation.89 | convolution fusion | flops 471252992 | bytes 4259840 | tf_op jit(solution)/shard_map/dot_general | solution.py:434
  155.1 1.7 fusion.2
  156.9 35.1 %shard_map.130 = (bf16[4,4,16,2048]{3,2,1,0:T(8,128)(2,1)}, bf16[2,256,448]{2,1,0:T(8,128)(2,1)}, bf16[2,256,448]{2,1,0:T(8,128)(2,1)}, bf16[2,256,448]{2,1,0:T(...) custom-call(bf16[4,4,16,2048]{3,2,1,0:T(8,128)(2,1)} %bitcast.192, ...), custom_call_target="tpu_custom_call" | custom-call | bytes 33554432 | tf_op jit(solution)/shard_map/pallas_call | solution.py:169
  191.9 3.4 %multiply_convert_fusion = (bf16[256,448]{1,0:T(8,128)(2,1)}, bf16[256,448]{1,0:T(8,128)(2,1)}) fusion(f32[256,448]{1,0:T(8,128)S(1)} %copy-done.41, f32[256,448]{1,0:T(8,128)S(1)} %copy-done.44, bf16[256,2048]{1,0:T(8,128)(2,1)} %bitcast.197, bf16[2,448,2048]{2,1,0:T(8,128)(2,1)} %param.11), kind=kOutput, calls=%fused_computation.87 | convolution fusion | flops 471252992 | bytes 4259840 | tf_op jit(solution)/shard_map/dot_general | solution.py:434
  195.4 5.5 %shard_map.131 = (bf16[2,256,448]{2,1,0:T(8,128)(2,1)}, bf16[2,256,448]{2,1,0:T(8,128)(2,1)}, bf16[2,256,1024]{2,1,0:T(8,128)(2,1)}) custom-call(bf16[256,448]{1,0:T(8,128)(2,1)} %get-tuple-element.55.refs_0_, bf16[256,448]{1,0:T(8,128)(2,1)} %get-tuple-element.54.refs_1_, bf16[256,2048]{1,0:T(8,128)(2,1)} %bitcast.198), custom_call_target="tpu_custom_call" | custom-call | tf_op jit(solution)/shard_map/pallas_call | solution.py:215
  200.9 1.8 convolution_bitcast_fusion.5.refs_0_
  207.0 1.9 copy-done.22
  212.1 15.4 %shard_map.132 = f32[8,128]{1,0:T(8,128)S(1)} custom-call(f32[8,1024]{1,0:T(8,128)S(1)} %get-tuple-element.27.norm, f32[1,1]{1,0:T(1,128)} %bitcast.174.damping, f32[2,448,1024]{2,1,0:T(8,128)S(1)} %bitcast.179, f32[2,448,1024]{2,1,0:T(8,128)S(1)} %bitcast.176, f32[2,448,1024]{2,1,0:T(8,128)S(1)} %copy-done, ...), custom_call_target="tpu_custom_call" | custom-call | tf_op jit(solution)/shard_map/pallas_call | solution.py:399
  228.2 8.6 %fusion.8 = (f32[1,448,1024]{2,1,0:T(8,128)}, f32[1,448,1024]{2,1,0:T(8,128)}, f32[1,448,1024]{2,1,0:T(8,128)}, f32[1,448,1024]{2,1,0:T(8,128)}) fusion(f32[2,448,1024]{2,1,0:T(8,128)S(1)} %bitcast.177, f32[448,1024]{1,0:T(8,128)} %copy-done.5, f32[]{:T(128)} %bitcast.28, f32[]{:T(128)} %bitcast.26, f32[448,1024]{1,0:T(8,128)} %copy-done.8, ...), kind=kLoop, calls=%fused_computation.17 | loop fusion | flops 5505024 | bytes 22020104 | tf_op jit(solution)/shard_map/stack | solution.py:495
  236.8 4.7 %fusion.16 = (f32[1,448,1024]{2,1,0:T(8,128)S(1)}, f32[1,448,1024]{2,1,0:T(8,128)S(1)}) fusion(f32[448,1024]{1,0:T(8,128)} %copy-done.3, f32[2,448,1024]{2,1,0:T(8,128)S(1)} %copy-done, f32[]{:T(128)} %bitcast.28, f32[]{:T(128)} %bitcast.26, f32[448,1024]{1,0:T(8,128)} %copy-done.6), kind=kLoop, calls=%fused_computation.29 | loop fusion | flops 2752512 | bytes 11010056 | tf_op jit(solution)/shard_map/stack | solution.py:495
  241.5 2.3 maximum_bitcast_fusion.1
  244.9 2.3 maximum_bitcast_fusion
  247.1 4.9 %pad_maximum_fusion = (f32[2,448,1024]{2,1,0:T(8,128)}, f32[2,448,1024]{2,1,0:T(8,128)}) fusion(f32[1,448,1024]{2,1,0:T(8,128)S(1)} %get-tuple-element.49, f32[1,448,1024]{2,1,0:T(8,128)S(1)} %get-tuple-element.48, f32[2,448,1024]{2,1,0:T(8,128)S(1)} %copy-done, f32[]{:T(128)} %bitcast.25), kind=kLoop, calls=%fused_computation.2 | loop fusion | flops 1835008 | bytes 14680068 | tf_op jit(solution)/shard_map/stack | solution.py:495
  252.1 4.6 %broadcast_multiply_fusion.1 = (f32[2,1024,448]{1,2,0:T(8,128)}, f32[2,1024,448]{1,2,0:T(8,128)}) fusion(f32[2,1024,448]{1,2,0:T(8,128)S(1)} %copy-done.1, f32[]{:T(128)} %bitcast.25, f32[2,1024,448]{1,2,0:T(8,128)S(1)} %copy-done.2), kind=kLoop, calls=%fused_computation.55 | loop fusion | flops 1835008 | bytes 14680068 | tf_op jit(solution)/shard_map/mul | solution.py:493
  (105 shorter events, 24.7 us)
Async XLA Ops:
  2.1 23.2 %copy-start.28 = (bf16[2,2048,448]{1,2,0:T(8,128)(2,1)S(1)}, bf16[2,2048,448]{1,2,0:T(8,128)(2,1)}, u32[]{:S(2)}) copy-start(bf16[2,2048,448]{1,2,0:T(8,128)(2,1)} %param.9) | copy-start | bytes 11010052
  28.1 10.9 %copy-start.18 = (bf16[256,448]{1,0:T(8,128)(2,1)}, bf16[256,448]{1,0:T(8,128)(2,1)S(1)}, u32[]{:S(2)}) copy-start(bf16[256,448]{1,0:T(8,128)(2,1)S(1)} %get-tuple-element.63.refs_5_) | copy-start | bytes 688132
  35.0 4.0 %copy-start.36 = (bf16[2,448,2048]{2,1,0:T(8,128)(2,1)S(1)}, bf16[2,448,2048]{2,1,0:T(8,128)(2,1)}, u32[]{:S(2)}) copy-start(bf16[2,448,2048]{2,1,0:T(8,128)(2,1)} %param.11) | copy-start | bytes 11010052
  42.0 58.6 %copy-start.37 = (bf16[448,2048]{1,0:T(8,128)(2,1)S(1)}, bf16[448,2048]{1,0:T(8,128)(2,1)}, u32[]{:S(2)}) copy-start(bf16[448,2048]{1,0:T(8,128)(2,1)} %get-tuple-element.34) | copy-start | bytes 5505028
  97.8 4.3 %copy-start.29 = (bf16[2,2048,448]{1,2,0:T(8,128)(2,1)S(1)}, bf16[2,2048,448]{1,2,0:T(8,128)(2,1)}, u32[]{:S(2)}) copy-start(bf16[2,2048,448]{1,2,0:T(8,128)(2,1)} %param.9) | copy-start | bytes 11010052
  106.6 5.9 %copy-start.19 = (bf16[256,448]{1,0:T(8,128)(2,1)}, bf16[256,448]{1,0:T(8,128)(2,1)S(1)}, u32[]{:S(2)}) copy-start(bf16[256,448]{1,0:T(8,128)(2,1)S(1)} %get-tuple-element.65.refs_4_) | copy-start | bytes 688132
  106.6 5.9 %copy-start.16 = (bf16[448,2048]{1,0:T(8,128)(2,1)S(1)}, bf16[448,2048]{1,0:T(8,128)(2,1)}, u32[]{:S(2)}) copy-start(bf16[448,2048]{1,0:T(8,128)(2,1)} %get-tuple-element.36) | copy-start | bytes 5505028
  115.9 33.1 %copy-start.39 = (f32[256,448]{1,0:T(8,128)S(1)}, f32[256,448]{1,0:T(8,128)}, u32[]{:S(2)}) copy-start(f32[256,448]{1,0:T(8,128)} %copy-done.38) | copy-start | bytes 1376260
  115.9 33.1 %copy-start.42 = (f32[256,448]{1,0:T(8,128)S(1)}, f32[256,448]{1,0:T(8,128)}, u32[]{:S(2)}) copy-start(f32[256,448]{1,0:T(8,128)} %get-tuple-element.66) | copy-start | bytes 1376260
  149.0 4.1 %copy-start.30 = (bf16[2,2048,448]{1,2,0:T(8,128)(2,1)S(1)}, bf16[2,2048,448]{1,2,0:T(8,128)(2,1)}, u32[]{:S(2)}) copy-start(bf16[2,2048,448]{1,2,0:T(8,128)(2,1)} %param.9) | copy-start | bytes 11010052
  156.8 35.1 %copy-start.41 = (f32[256,448]{1,0:T(8,128)S(1)}, f32[256,448]{1,0:T(8,128)}, u32[]{:S(2)}) copy-start(f32[256,448]{1,0:T(8,128)} %copy-done.40) | copy-start | bytes 1376260
  156.9 35.1 %copy-start.44 = (f32[256,448]{1,0:T(8,128)S(1)}, f32[256,448]{1,0:T(8,128)}, u32[]{:S(2)}) copy-start(f32[256,448]{1,0:T(8,128)} %copy-done.43) | copy-start | bytes 1376260
  195.4 5.5 %copy-start.15 = (bf16[2,256,1024]{2,1,0:T(8,128)(2,1)S(1)}, bf16[2,256,1024]{2,1,0:T(8,128)(2,1)}, u32[]{:S(2)}) copy-start(bf16[2,256,1024]{2,1,0:T(8,128)(2,1)} %get-tuple-element.39) | copy-start | bytes 3145732
  202.7 7.1 %copy-start.4 = (f32[448,1024]{1,0:T(8,128)}, f32[448,1024]{1,0:T(8,128)S(1)}, u32[]{:S(2)}) copy-start(f32[448,1024]{1,0:T(8,128)S(1)} %convolution_bitcast_fusion.5.refs_0_) | copy-start | bytes 5505028
  204.7 5.1 %copy-start.5 = (f32[448,1024]{1,0:T(8,128)}, f32[448,1024]{1,0:T(8,128)S(1)}, u32[]{:S(2)}) copy-start(f32[448,1024]{1,0:T(8,128)S(1)} %convolution_bitcast_fusion.4.refs_1_) | copy-start | bytes 5505028
  204.7 5.1 %copy-start.2 = (f32[2,1024,448]{1,2,0:T(8,128)S(1)}, f32[2,1024,448]{1,2,0:T(8,128)}, u32[]{:S(2)}) copy-start(f32[2,1024,448]{1,2,0:T(8,128)} %param.12) | copy-start | bytes 11010052
  205.6 22.0 %copy-start.3 = (f32[448,1024]{1,0:T(8,128)}, f32[448,1024]{1,0:T(8,128)S(1)}, u32[]{:S(2)}) copy-start(f32[448,1024]{1,0:T(8,128)S(1)} %convolution_bitcast_fusion.3.refs_2_) | copy-start | bytes 5505028
  205.7 3.4 %copy-start.31 = (bf16[2,256,448]{2,1,0:T(8,128)(2,1)S(1)}, bf16[2,256,448]{2,1,0:T(8,128)(2,1)}, u32[]{:S(2)}) copy-start(bf16[2,256,448]{2,1,0:T(8,128)(2,1)} %get-tuple-element.46) | copy-start | bytes 1376260
  205.7 5.5 %copy-start.1 = (f32[2,1024,448]{1,2,0:T(8,128)S(1)}, f32[2,1024,448]{1,2,0:T(8,128)}, u32[]{:S(2)}) copy-start(f32[2,1024,448]{1,2,0:T(8,128)} %param.13) | copy-start | bytes 11010052
  206.4 5.8 %copy-start = (f32[2,448,1024]{2,1,0:T(8,128)S(1)}, f32[2,448,1024]{2,1,0:T(8,128)}, u32[]{:S(2)}) copy-start(f32[2,448,1024]{2,1,0:T(8,128)} %down.3) | copy-start | bytes 11010052
  209.1 18.5 %copy-start.8 = (f32[448,1024]{1,0:T(8,128)}, f32[448,1024]{1,0:T(8,128)S(1)}, u32[]{:S(2)}) copy-start(f32[448,1024]{1,0:T(8,128)S(1)} %convolution_bitcast_fusion.1.refs_4_) | copy-start | bytes 5505028
  212.1 15.5 %copy-start.6 = (f32[448,1024]{1,0:T(8,128)}, f32[448,1024]{1,0:T(8,128)S(1)}, u32[]{:S(2)}) copy-start(f32[448,1024]{1,0:T(8,128)S(1)} %convolution_bitcast_fusion.refs_5_) | copy-start | bytes 5505028
  236.8 4.7 %copy-start.12 = (f32[1,448,1024]{2,1,0:T(8,128)S(1)}, f32[1,448,1024]{2,1,0:T(8,128)}, u32[]{:S(2)}) copy-start(f32[1,448,1024]{2,1,0:T(8,128)} %get-tuple-element.50) | copy-start | bytes 5505028
  236.8 4.7 %copy-start.13 = (f32[1,448,1024]{2,1,0:T(8,128)S(1)}, f32[1,448,1024]{2,1,0:T(8,128)}, u32[]{:S(2)}) copy-start(f32[1,448,1024]{2,1,0:T(8,128)} %get-tuple-element.51) | copy-start | bytes 5505028
  (21 other events, 44.2 us)

commit v3 on v2

--- a/solution.py
+++ b/solution.py
@@ -6,7 +6,7 @@
 from jax.experimental.pallas import tpu as pltpu
 from jax.sharding import PartitionSpec as P
 
-ITERS = 1
+LIMIT = 24 * 1024 * 1024
 MESH = pl.DeviceIdType.MESH
 
 
@@ -79,79 +79,133 @@
     base += count
     pairs = refs[base:base + paired]
     base += paired
-    near_slots, held, far_slots, s1s, s1r, s2s, s2r, g1s, g1r, g2s, g2r = refs[base:base + 11]
+    lanes = lanes_of(outer, inner, parts[0].shape[-1], refs[base:])
     far, near, along_outer, along_inner = place(outer, inner)
     peers = [along_outer(e) for e in range(1, outer)] + [along_inner(d) for d in range(1, inner)]
     if paired:
         peers.append({"dp": 1 - lax.axis_index("dp")})
     greet(peers)
-    order = list(range(1, outer)) + [0]
-    copies = []
-    first, second, third, fourth = {}, {}, {}, {}
-    for e in order:
-        piece = lax.rem(far + e, outer)
+    sent = []
+
+    def roles(lane):
+        if lane["far_first"]:
+            return far, near, along_outer, along_inner
+        return near, far, along_inner, along_outer
+
+    def spot(ref, lane, one, two):
+        index = (two, one) if lane["far_first"] else (one, two)
+        return ref.at[index[0], index[1], :, lane["columns"]]
+
+    def launch(*call):
+        copy = remote(*call)
+        sent.append(copy)
+        return copy
+
+    first, second, third, fourth, own = {}, {}, {}, {}, {}
+    for lane in lanes:
+        one, two, along_one, along_two = roles(lane)
+        for e in lane["order"]:
+            piece = lax.rem(two + e, lane["twos"])
+            for k in range(count):
+                for d in range(1, lane["ones"]):
+                    target = lax.rem(one + d, lane["ones"])
+                    first[lane["name"], k, d, e] = launch(
+                        spot(parts[k], lane, target, piece), lane["slots"].at[k, d, e],
+                        lane["s1s"].at[k, d, e], lane["s1r"].at[k, d, e], along_one(d),
+                    )
+    swaps = start_pairs(sources, pairs, *refs[base + 22:]) if paired else []
+    keep_pairs(sources, pairs)
+    for turn in range(max(outer, inner)):
+        for lane in lanes:
+            if turn >= lane["twos"]:
+                continue
+            e = lane["order"][turn]
+            one, two, along_one, along_two = roles(lane)
+            piece = lax.rem(two + e, lane["twos"])
+            for k in range(count):
+                total = spot(parts[k], lane, one, piece)[...].astype(jnp.float32)
+                for d in range(1, lane["ones"]):
+                    first[lane["name"], k, d, e].wait_recv()
+                    total = total + lane["slots"][k, d, e].astype(jnp.float32)
+                if e:
+                    lane["held"][k, e] = total.astype(jnp.bfloat16)
+                    second[lane["name"], k, e] = launch(
+                        lane["held"].at[k, e], lane["ends"].at[k, e],
+                        lane["s2s"].at[k, e], lane["s2r"].at[k, e], along_two(e),
+                    )
+                else:
+                    own[lane["name"], k] = total
+    for lane in lanes:
+        one, two, along_one, along_two = roles(lane)
         for k in range(count):
-            for d in range(1, inner):
-                first[k, d, e] = remote(
-                    parts[k].at[lax.rem(near + d, inner), piece], near_slots.at[k, d, e],
-                    s1s.at[k, d, e], s1r.at[k, d, e], along_inner(d),
+            total = own[lane["name"], k]
+            for e in range(1, lane["twos"]):
+                second[lane["name"], k, e].wait_recv()
+                total = total + lane["ends"][k, e].astype(jnp.float32)
+            if k in extra:
+                total = total + spot(extra[k], lane, one, two)[...].astype(jnp.float32)
+            block = spot(outs[k], lane, one, two)
+            block[...] = total.astype(jnp.bfloat16)
+            for e in range(1, lane["twos"]):
+                third[lane["name"], k, e] = launch(
+                    block, block, lane["g1s"].at[k, e], lane["g1r"].at[k, e], along_two(e)
                 )
-    swaps = start_pairs(sources, pairs, *refs[base + 11:]) if paired else []
-    keep_pairs(sources, pairs)
-    own = {}
-    for e in order:
-        piece = lax.rem(far + e, outer)
-        for k in range(count):
-            total = parts[k][near, piece].astype(jnp.float32)
-            for d in range(1, inner):
-                first[k, d, e].wait_recv()
-                total = total + near_slots[k, d, e].astype(jnp.float32)
-            if e:
-                held[k, e] = total.astype(jnp.bfloat16)
-                second[k, e] = remote(
-                    held.at[k, e], far_slots.at[k, e], s2s.at[k, e], s2r.at[k, e], along_outer(e)
+            for d in range(1, lane["ones"]):
+                fourth[lane["name"], k, d, 0] = launch(
+                    block, block, lane["g2s"].at[k, d, 0], lane["g2r"].at[k, d, 0], along_one(d)
                 )
-            else:
-                own[k] = total
-    for k in range(count):
-        total = own[k]
-        for e in range(1, outer):
-            second[k, e].wait_recv()
-            total = total + far_slots[k, e].astype(jnp.float32)
-        if k in extra:
-            total = total + extra[k][near, far].astype(jnp.float32)
-        outs[k][near, far] = total.astype(jnp.bfloat16)
-        spread(outer, inner, outs[k], far, near, along_outer, along_inner, third, fourth, k,
-               g1s, g1r, g2s, g2r)
-    forward(outer, inner, outs, far, near, along_inner, third, fourth, g2s, g2r)
+    for e in range(1, max(outer, inner)):
+        for lane in lanes:
+            if e >= lane["twos"]:
+                continue
+            one, two, along_one, along_two = roles(lane)
+            piece = lax.rem(two - e + lane["twos"], lane["twos"])
+            for k in range(count):
+                third[lane["name"], k, e].wait_recv()
+                block = spot(outs[k], lane, one, piece)
+                for d in range(1, lane["ones"]):
+                    fourth[lane["name"], k, d, e] = launch(
+                        block, block, lane["g2s"].at[k, d, e], lane["g2r"].at[k, d, e], along_one(d)
+                    )
+    for copy in fourth.values():
+        copy.wait_recv()
     for copy in swaps:
         copy.wait()
-    for table in (first, second, third, fourth):
-        for copy in table.values():
-            copy.wait_send()
-
-
-def spread(outer, inner, out, far, near, along_outer, along_inner, third, fourth, k, g1s, g1r, g2s, g2r):
-    for e in range(1, outer):
-        third[k, e] = remote(out.at[near, far], out.at[near, far], g1s.at[k, e], g1r.at[k, e], along_outer(e))
-    for d in range(1, inner):
-        fourth[k, d, 0] = remote(
-            out.at[near, far], out.at[near, far], g2s.at[k, d, 0], g2r.at[k, d, 0], along_inner(d)
+    for copy in sent:
+        copy.wait_send()
+
+
+def cut_of(width):
+    return max(width * 13 // 16 // 128 * 128, 128)
+
+
+def lane_scratch(count, ones, twos, share, width):
+    dma = pltpu.SemaphoreType.DMA
+    return [
+        pltpu.VMEM((count, ones, twos, share, width), jnp.bfloat16),
+        pltpu.VMEM((count, twos, share, width), jnp.bfloat16),
+        pltpu.VMEM((count, twos, share, width), jnp.bfloat16),
+        dma((count, ones, twos)), dma((count, ones, twos)),
+        dma((count, twos)), dma((count, twos)),
+        dma((count, twos)), dma((count, twos)),
+        dma((count, ones, twos)), dma((count, ones, twos)),
+    ]
+
+
+def lanes_of(outer, inner, width, refs):
+    cut = cut_of(width)
+    names = ("slots", "held", "ends", "s1s", "s1r", "s2s", "s2r", "g1s", "g1r", "g2s", "g2r")
+    lanes = []
+    for far_first in (True, False):
+        ones, twos = (outer, inner) if far_first else (inner, outer)
+        lane = dict(zip(names, refs[11 * far_first:]))
+        lane.update(
+            name=int(far_first), far_first=far_first, ones=ones, twos=twos,
+            order=list(range(1, twos)) + [0],
+            columns=pl.ds(cut, width - cut) if far_first else pl.ds(0, cut),
         )
-
-
-def forward(outer, inner, outs, far, near, along_inner, third, fourth, g2s, g2r):
-    for e in range(1, outer):
-        piece = lax.rem(far - e + outer, outer)
-        for k in range(len(outs)):
-            third[k, e].wait_recv()
-            for d in range(1, inner):
-                fourth[k, d, e] = remote(
-                    outs[k].at[near, piece], outs[k].at[near, piece],
-                    g2s.at[k, d, e], g2r.at[k, d, e], along_inner(d),
-                )
-    for copy in fourth.values():
-        copy.wait_recv()
+        lanes.append(lane)
+    return lanes
 
 
 def summed_whole(mp, parts, adds, ident, full=(), half=()):
@@ -168,22 +222,15 @@
     operands += list(full) + list(half)
     outs = pl.pallas_call(
         functools.partial(sum_kernel, outer, inner, count, which, paired),
-        out_shape=[jax.ShapeDtypeStruct(view, jnp.bfloat16)] * count + pair_shapes(full, half),
+        out_shape=[pltpu.VMEM(view, jnp.bfloat16)] * count + pair_shapes(full, half),
         in_specs=[pl.BlockSpec(memory_space=pltpu.VMEM)] * len(operands),
         out_specs=[pl.BlockSpec(memory_space=pltpu.VMEM)] * (count + paired),
-        scratch_shapes=[
-            pltpu.VMEM((count, inner, outer, share, width), jnp.bfloat16),
-            pltpu.VMEM((count, outer, share, width), jnp.bfloat16),
-            pltpu.VMEM((count, outer, share, width), jnp.bfloat16),
-            dma((count, inner, outer)), dma((count, inner, outer)),
-            dma((count, outer)), dma((count, outer)),
-            dma((count, outer)), dma((count, outer)),
-            dma((count, inner, outer)), dma((count, inner, outer)),
-        ] + [dma((paired,))] * (2 if paired else 0),
-        cost_estimate=pl.CostEstimate(
-            flops=0, bytes_accessed=count * rows * width * 64, transcendentals=0
+        scratch_shapes=lane_scratch(count, inner, outer, share, cut_of(width))
+        + lane_scratch(count, outer, inner, share, width - cut_of(width))
+        + [dma((paired,))] * (2 if paired else 0),
+        compiler_params=pltpu.CompilerParams(
+            collective_id=ident, has_side_effects=True, vmem_limit_bytes=LIMIT
         ),
-        compiler_params=pltpu.CompilerParams(collective_id=ident, has_side_effects=True),
     )(*operands)
     return [o.reshape(rows, width) for o in outs[:count]] + joined(outs[count:])
 
@@ -218,7 +265,9 @@
             in_specs=spec,
             out_specs=spec,
             scratch_shapes=[dma((paired,)), dma((paired,))],
-            compiler_params=pltpu.CompilerParams(collective_id=ident, has_side_effects=True),
+            compiler_params=pltpu.CompilerParams(
+                collective_id=ident, has_side_effects=True, vmem_limit_bytes=LIMIT // 2
+            ),
         )(*full, *half)
     )
 
@@ -327,7 +376,8 @@
 
 
 def scalar_kernel(dp, mp, scale, norm, damping, gate, up, down, *refs):
-    grads, (out, right, held, packed, slots, loads, send, receive) = refs[:6], refs[6:]
+    grads, out, rights, helds = refs[:6], refs[6], refs[7:10], refs[10:13]
+    packed, slots, loads, send, receive = refs[13:]
     row, column = lax.axis_index("dp"), lax.axis_index("mp")
     total = dp * mp
     me = row * mp + column
@@ -344,13 +394,13 @@
     for k, (source, layer) in enumerate(blocks):
         fetches.append(
             (
-                pltpu.make_async_copy(source.at[layer], right.at[k], loads.at[k, 0]),
-                pltpu.make_async_copy(grads[k], held.at[k], loads.at[k, 1]),
+                pltpu.make_async_copy(source.at[layer], rights[k % 3].at[layer], loads.at[k, 0]),
+                pltpu.make_async_copy(grads[k], helds[k % 3].at[layer], loads.at[k, 1]),
             )
         )
         for fetch in fetches[k]:
             fetch.start()
-    rows, width = right.shape[1:]
+    rows, width = rights[0].shape[1:]
     chunk = chunk_of(rows)
     zero = jnp.zeros((8, width), jnp.float32)
     sums = (zero, zero)
@@ -360,7 +410,7 @@
 
         def piece(step, carry):
             span = pl.ds(pl.multiple_of(step * chunk, chunk), chunk)
-            value, grad = right[k, span], held[k, span]
+            value, grad = rights[k % 3][k // 3, span], helds[k % 3][k // 3, span]
             return carry[0] + folded(value * grad), carry[1] + folded(grad * grad)
 
         sums = lax.fori_loop(0, rows // chunk, piece, sums)
@@ -396,14 +446,13 @@
     hidden, width = rhs[0].shape[1:]
     dma = pltpu.SemaphoreType.DMA
     vmem, anywhere = pl.BlockSpec(memory_space=pltpu.VMEM), pl.BlockSpec(memory_space=pl.ANY)
-    out = pl.pallas_call(
+    out, *kept = pl.pallas_call(
         functools.partial(scalar_kernel, dp, mp, scale),
-        out_shape=jax.ShapeDtypeStruct((8, 128), jnp.float32),
+        out_shape=[jax.ShapeDtypeStruct((8, 128), jnp.float32)]
+        + [pltpu.VMEM((2, hidden, width), jnp.float32)] * 6,
         in_specs=[vmem, vmem] + [anywhere] * 9,
-        out_specs=vmem,
+        out_specs=[vmem] * 7,
         scratch_shapes=[
-            pltpu.VMEM((6, hidden, width), jnp.float32),
-            pltpu.VMEM((6, hidden, width), jnp.float32),
             pltpu.VMEM((3, 8, 128), jnp.float32),
             pltpu.VMEM((total, 3, 8, 128), jnp.float32),
             dma((6, 2)), dma((total,)), dma((total,)),
@@ -412,7 +461,52 @@
             collective_id=ident, has_side_effects=True, vmem_limit_bytes=32 * 1024 * 1024
         ),
     )(norm, damping.reshape(1, 1), *rhs, *grads)
-    return out[0, 0], out[1, 0], out[2, 0]
+    return out, kept[:3], kept[3:]
+
+
+def finish_kernel(factors, *refs):
+    rights, helds, outs, sems = refs[:3], refs[3:6], refs[6:12], refs[12:]
+    steps, nexts, sem = sems
+    alpha, keep, drop = (factors[k:k + 1, :1] for k in range(3))
+    rows, width = rights[0].shape[1:]
+    chunk = chunk_of(rows)
+    copies = []
+    for k in range(6):
+        which, layer = k % 3, k // 3
+
+        def piece(step, carry):
+            span = pl.ds(pl.multiple_of(step * chunk, chunk), chunk)
+            value = rights[which][layer, span]
+            steps[k, span] = alpha * value
+            nexts[k, span] = keep * value - drop * helds[which][layer, span]
+            return carry
+
+        lax.fori_loop(0, rows // chunk, piece, 0)
+        for place_of, (source, target) in enumerate(
+            ((steps, outs[which]), (nexts, outs[3 + which]))
+        ):
+            copy = pltpu.make_async_copy(source.at[k], target.at[layer], sem.at[k, place_of])
+            copy.start()
+            copies.append(copy)
+    for copy in copies:
+        copy.wait()
+
+
+def finished(factors, rights, helds):
+    shape = rights[0].shape
+    vmem, anywhere = pl.BlockSpec(memory_space=pltpu.VMEM), pl.BlockSpec(memory_space=pl.ANY)
+    return pl.pallas_call(
+        finish_kernel,
+        out_shape=[pltpu.HBM(shape, jnp.float32)] * 6,
+        in_specs=[vmem] * 7,
+        out_specs=[anywhere] * 6,
+        scratch_shapes=[
+            pltpu.VMEM((6,) + shape[1:], jnp.float32),
+            pltpu.VMEM((6,) + shape[1:], jnp.float32),
+            pltpu.SemaphoreType.DMA((6, 2)),
+        ],
+        compiler_params=pltpu.CompilerParams(vmem_limit_bytes=26 * 1024 * 1024),
+    )(factors, *rights, *helds)
 
 
 def silu_terms(value):
@@ -488,13 +582,11 @@
     back_up = (back_hidden * active_one).astype(jnp.bfloat16)
     gates, ups, backs = swapped((back_gate, back_up), (back_layer,), 5)
     first = (rows_product(gates, inputs), rows_product(ups, inputs), rows_product(first_hiddens, backs))
-    grads = (first, second)
-    alpha, keep, drop = coefficients(dp, mp, scale, norm, damping, turned, first + second, 4)
-    steps = [alpha * turned[k] for k in range(3)]
-    nexts = [
-        jnp.stack([keep * turned[k][layer] - drop * grads[layer][k] for layer in range(2)])
-        for k in range(3)
-    ]
+    factors, rights, helds = coefficients(
+        dp, mp, scale, norm, damping, turned, first + second, 4
+    )
+    outs = finished(factors, rights, helds)
+    steps, nexts = list(outs[:3]), list(outs[3:])
     for arrays in (steps, nexts):
         arrays[0], arrays[1] = arrays[0].transpose(0, 2, 1), arrays[1].transpose(0, 2, 1)
     return tuple(steps) + tuple(nexts)

time: 257 us -> 215 us (0.84)
  other arithmetic: 27.4 us -> 0 us
  Pallas kernels: 167 us -> 159 us
  matrix products: 44.5 us -> 41.3 us
  local copies, waits for them, and re-layouts: 15.6 us -> 12.5 us
    pallas_call x3, Pallas kernels: 124 us -> 105 us  [summed_whole(): pl.pallas_call(functools.partial(sum_kernel, outer, inner, count, which,...]
    another operation x3 -> x0, other arithmetic: 18.2 us -> none  [body(): jnp.stack([keep * turned[k][layer] - drop * grads[layer][k] for layer in...]
    pallas_call x0 -> x1, Pallas kernels: none -> 8.22 us  [finished(): pl.pallas_call(finish_kernel, out_shape=[pltpu.HBM(shape, jnp.float32)] *...]
    dot_general x7, matrix products: 14.5 us -> 7.23 us  [against(): lax.dot_general(left, right, (((1,), (1,)), ((), ())), preferred_element_...]
    dot_general x6, matrix products: 5.29 us -> 11.4 us  [rows_product(): lax.dot_general(left, right, (((0,), (0,)), ((), ())), preferred_element_...]
    pallas_call x1, Pallas kernels: 15.4 us -> 20.6 us  [coefficients(): pl.pallas_call(functools.partial(scalar_kernel, dp, mp, scale), out_shape...]
    mul x1 -> x0, other arithmetic: 4.62 us -> none  [body(): steps = [alpha * turned[k] for k in range(3)]]
    transpose x2 -> x0, other arithmetic: 4.59 us -> none  [the longest x1 2.32 us: body(): arrays[1].transpose(0, 2, 1)]
where the time goes in v3:
time: 215 us
  Pallas kernels  159 us (74%)
  matrix products  41.3 us (19%)
  local copies, waits for them, and re-layouts  12.5 us (6%)
    pallas_call x3, Pallas kernels, summed_whole(): pl.pallas_call(functools.partial(sum_kernel, outer, inner, count, which,...  105 us
    dot_general x10, matrix products, matmul(): return jnp.dot(left, right, preferred_element_type=jnp.float32)  22.7 us
    pallas_call x1, Pallas kernels, gathered(): pl.pallas_call(functools.partial(gather_kernel, outer, inner), out_shape=...  22.6 us
    pallas_call x1, Pallas kernels, coefficients(): pl.pallas_call(functools.partial(scalar_kernel, dp, mp, scale), out_shape...  20.6 us
    dot_general x6, matrix products, rows_product(): lax.dot_general(left, right, (((0,), (0,)), ((), ())), preferred_element_...  11.4 us
    unnamed x49, local copies, waits for them, and re-layouts  11.2 us
    pallas_call x1, Pallas kernels, finished(): pl.pallas_call(finish_kernel, out_shape=[pltpu.HBM(shape, jnp.float32)] *...  8.22 us
    dot_general x7, matrix products, against(): lax.dot_general(left, right, (((1,), (1,)), ((), ())), preferred_element_...  7.23 us

profile of v3, /device:TPU:0, one launch (start us, length us, event | category | flops | bytes accessed | tf_op | source)
XLA Modules:
  0.0 214.5 jit_solution(3130397259016189751)
XLA Ops:
  2.1 22.6 %shard_map.127 = (bf16[4,4,256,128]{3,2,1,0:T(8,128)(2,1)S(1)}, f32[8,1024]{1,0:T(8,128)S(1)}, bf16[448,2048]{1,0:T(8,128)(2,1)S(1)}, bf16[448,2048]{1,0:T(8,128...) custom-call(bf16[256,128]{1,0:T(8,128)(2,1)S(1)} %copy-done.3, ...), custom_call_target="tpu_custom_call" | custom-call | tf_op jit(solution)/shard_map/pallas_call | solution.py:357
  26.2 1.7 copy-done.7
  29.4 1.6 convolution_multiply_fusion.1
  30.9 4.6 %fusion.20 = f32[256,2048]{1,0:T(8,128)} fusion(bf16[2,448,2048]{2,1,0:T(8,128)(2,1)} %param.11, f32[256,448]{1,0:T(8,128)} %convolution_multiply_fusion.1, bf16[448,2048]{1,0:T(8,128)(2,1)S(1)} %get-tuple-element.43, f32[256,448]{1,0:T(8,128)} %copy-done.19, bf16[32,8,16,128]{3,2,1,0:T(8,128)(2,1)S(1)} %bitcast.152), kind=kOutput, calls=%fused_computation.24 | convolution fusion | flops 940326912 | bytes 7864320 | tf_op jit(solution)/shard_map/dot_general | solution.py:518
  35.5 3.0 %fusion = bf16[256,2048]{1,0:T(8,128)(2,1)S(1)} fusion(f32[256,2048]{1,0:T(8,128)} %fusion.20, bf16[256,448]{1,0:T(8,128)(2,1)S(1)} %get-tuple-element.80.refs_5_, bf16[448,2048]{1,0:T(8,128)(2,1)} %get-tuple-element.44), kind=kOutput, calls=%fused_computation.4 | convolution fusion | flops 470810624 | bytes 5210112 | tf_op jit(solution)/shard_map/dot_general | solution.py:518
  38.7 1.7 convolution_convert_fusion
  42.3 47.9 %shard_map.128 = (bf16[4,4,16,2048]{3,2,1,0:T(8,128)(2,1)S(1)}, bf16[4,4,16,2048]{3,2,1,0:T(8,128)(2,1)S(1)}) custom-call(bf16[4,4,16,2048]{3,2,1,0:T(8,128)(2,1)S(1)} %bitcast.136, bf16[4,4,16,2048]{3,2,1,0:T(8,128)(2,1)S(1)} %bitcast.130, bf16[4,4,16,2048]{3,2,1,0:T(8,128)(2,1)S(1)} %reshape_reshape.3.refs_2_), custom_call_target="tpu_custom_call" | custom-call | tf_op jit(solution)/shard_map/pallas_call | solution.py:223
  92.2 1.6 fusion.66
  95.1 1.3 copy-done.8
  96.4 1.6 fusion.52
  98.1 1.6 multiply_convert_fusion.4
  99.6 5.6 %fusion.5 = f32[256,2048]{1,0:T(8,128)} fusion(bf16[2,448,2048]{2,1,0:T(8,128)(2,1)} %param.11, f32[256,448]{1,0:T(8,128)} %fusion.52, f32[256,448]{1,0:T(8,128)} %fusion.66, bf16[256,2048]{1,0:T(8,128)(2,1)S(1)} %bitcast.135, bf16[2,2048,448]{1,2,0:T(8,128)(2,1)} %param.9, f32[256,448]{1,0:T(8,128)} %get-tuple-element.83, f32[256,448]{1,0:T(8,128)} %copy-done.17), kind=kOutput, calls=%fused_computation.9 | convolution fusion | flops 940900352 | bytes 8912896 | tf_op jit(solution)/shard_map/dot_general | solution.py:518
  105.3 2.5 %fusion.1 = bf16[256,2048]{1,0:T(8,128)(2,1)S(1)} fusion(f32[256,2048]{1,0:T(8,128)} %fusion.5, bf16[256,448]{1,0:T(8,128)(2,1)S(1)} %get-tuple-element.82.refs_4_, bf16[448,2048]{1,0:T(8,128)(2,1)S(1)} %copy-done.6), kind=kOutput, calls=%fused_computation.5 | convolution fusion | flops 470810624 | bytes 5210112 | tf_op jit(solution)/shard_map/dot_general | solution.py:518
  107.7 29.1 %shard_map.129.refs_1_ = bf16[4,4,16,2048]{3,2,1,0:T(8,128)(2,1)S(1)} custom-call(bf16[4,4,16,2048]{3,2,1,0:T(8,128)(2,1)S(1)} %bitcast.131, bf16[4,4,16,2048]{3,2,1,0:T(8,128)(2,1)S(1)} %get-tuple-element.46.refs_1_), custom_call_target="tpu_custom_call" | custom-call | tf_op jit(solution)/shard_map/pallas_call | solution.py:223
  142.5 27.8 %shard_map.130 = (bf16[4,4,16,2048]{3,2,1,0:T(8,128)(2,1)S(1)}, bf16[2,256,448]{2,1,0:T(8,128)(2,1)S(1)}, bf16[2,256,448]{2,1,0:T(8,128)(2,1)S(1)}, bf16[2,256,4...) custom-call(bf16[4,4,16,2048]{3,2,1,0:T(8,128)(2,1)S(1)} %bitcast.13, ...), custom_call_target="tpu_custom_call" | custom-call | tf_op jit(solution)/shard_map/pallas_call | solution.py:223
  171.5 2.7 %shard_map.131 = (bf16[2,256,448]{2,1,0:T(8,128)(2,1)S(1)}, bf16[2,256,448]{2,1,0:T(8,128)(2,1)S(1)}, bf16[2,256,1024]{2,1,0:T(8,128)(2,1)S(1)}) custom-call(bf16[256,448]{1,0:T(8,128)(2,1)S(1)} %get-tuple-element.75.refs_0_, bf16[256,448]{1,0:T(8,128)(2,1)S(1)} %get-tuple-element.74.refs_1_, bf16[256,2048]{1,0:T(8,128)(2,1)S(1)} %bitcast.138), custom_call_target="tpu_custom_call" | custom-call | tf_op jit(solution)/shard_map/pallas_call | solution.py:262
  174.2 1.9 convolution_bitcast_fusion.5.refs_0_
  176.1 1.9 convolution_bitcast_fusion.4.refs_1_
  178.0 1.9 convolution_bitcast_fusion.3.refs_2_
  179.9 1.9 convolution_bitcast_fusion.2.refs_3_
  181.8 1.9 convolution_bitcast_fusion.1.refs_4_
  183.7 1.9 convolution_bitcast_fusion.refs_5_
  185.6 20.6 %shard_map.132 = (f32[8,128]{1,0:T(8,128)S(1)}, f32[2,448,1024]{2,1,0:T(8,128)S(1)}, f32[2,448,1024]{2,1,0:T(8,128)S(1)}, f32[2,448,1024]{2,1,0:T(8,128)S(1)}, f...) custom-call(f32[8,1024]{1,0:T(8,128)S(1)} %get-tuple-element.40.norm, ...), custom_call_target="tpu_custom_call" | custom-call | tf_op jit(solution)/shard_map/pallas_call | solution.py:449
  206.1 8.2 %shard_map.133 = (f32[2,448,1024]{2,1,0:T(8,128)}, f32[2,448,1024]{2,1,0:T(8,128)}, f32[2,448,1024]{2,1,0:T(8,128)}, f32[2,448,1024]{2,1,0:T(8,128)}, f32[2,448,1024]{2,1,0:T(8,128)}, /*index=5*/f32[2,448,1024]{2,1,0:T(8,128)}) custom-call(f32[8,128]{1,0:T(8,128)S(1)} %get-tuple-element.61.factors, f32[2,448,1024]{2,1,0:T(8,128)S(1)} %get-tuple-element.62.refs_0_, ...), custom_call_target="tpu_custom_call" | custom-call | tf_op jit(solution)/shard_map/pallas_call | solution.py:498
  (57 shorter events, 15.8 us)
Async XLA Ops:
  1.3 0.8 copy-start.3
  2.1 23.3 %copy-start.10 = (bf16[2,2048,448]{1,2,0:T(8,128)(2,1)S(1)}, bf16[2,2048,448]{1,2,0:T(8,128)(2,1)}, u32[]{:S(2)}) copy-start(bf16[2,2048,448]{1,2,0:T(8,128)(2,1)} %param.9) | copy-start | bytes 11010052
  25.4 15.0 %copy-start.4 = (bf16[16,256,128]{2,0,1:T(8,128)(2,1)}, bf16[16,256,128]{2,0,1:T(8,128)(2,1)S(1)}, u32[]{:S(2)}) copy-start(bf16[16,256,128]{2,0,1:T(8,128)(2,1)S(1)} %copy.61) | copy-start | bytes 3145732
  25.4 2.4 %copy-start.7 = (bf16[2,2048,448]{1,2,0:T(8,128)(2,1)S(1)}, bf16[2,2048,448]{1,2,0:T(8,128)(2,1)}, u32[]{:S(2)}) copy-start(bf16[2,2048,448]{1,2,0:T(8,128)(2,1)} %param.10) | copy-start | bytes 11010052
  27.8 0.8 copy-start.19
  28.6 0.8 copy-start.22
  35.5 3.2 %copy-start.13 = (bf16[2,448,2048]{2,1,0:T(8,128)(2,1)S(1)}, bf16[2,448,2048]{2,1,0:T(8,128)(2,1)}, u32[]{:S(2)}) copy-start(bf16[2,448,2048]{2,1,0:T(8,128)(2,1)} %param.11) | copy-start | bytes 11010052
  41.1 1.2 copy-start
  42.3 48.0 %copy-start.16 = (bf16[448,2048]{1,0:T(8,128)(2,1)S(1)}, bf16[448,2048]{1,0:T(8,128)(2,1)}, u32[]{:S(2)}) copy-start(bf16[448,2048]{1,0:T(8,128)(2,1)} %get-tuple-element.48) | copy-start | bytes 5505028
  90.3 7.8 %copy-start.1 = (bf16[4,4,16,2048]{3,2,1,0:T(8,128)(2,1)}, bf16[4,4,16,2048]{3,2,1,0:T(8,128)(2,1)S(1)}, u32[]{:S(2)}) copy-start(bf16[4,4,16,2048]{3,2,1,0:T(8,128)(2,1)S(1)} %get-tuple-element.45) | copy-start | bytes 3145732
  90.3 1.9 copy-start.15
  92.2 2.2 %copy-start.11 = (bf16[2,2048,448]{1,2,0:T(8,128)(2,1)S(1)}, bf16[2,2048,448]{1,2,0:T(8,128)(2,1)}, u32[]{:S(2)}) copy-start(bf16[2,2048,448]{1,2,0:T(8,128)(2,1)} %param.9) | copy-start | bytes 11010052
  94.4 2.0 copy-start.8
  96.4 1.6 copy-start.17
  99.6 5.6 %copy-start.6 = (bf16[448,2048]{1,0:T(8,128)(2,1)S(1)}, bf16[448,2048]{1,0:T(8,128)(2,1)}, u32[]{:S(2)}) copy-start(bf16[448,2048]{1,0:T(8,128)(2,1)} %get-tuple-element.49) | copy-start | bytes 5505028
  105.3 31.6 %copy-start.14 = (bf16[2,448,2048]{2,1,0:T(8,128)(2,1)S(1)}, bf16[2,448,2048]{2,1,0:T(8,128)(2,1)}, u32[]{:S(2)}) copy-start(bf16[2,448,2048]{2,1,0:T(8,128)(2,1)} %param.11) | copy-start | bytes 11010052
  107.7 29.2 %copy-start.18 = (f32[256,448]{1,0:T(8,128)S(1)}, f32[256,448]{1,0:T(8,128)}, u32[]{:S(2)}) copy-start(f32[256,448]{1,0:T(8,128)} %copy-done.17) | copy-start | bytes 1376260
  107.7 29.2 %copy-start.21 = (f32[256,448]{1,0:T(8,128)S(1)}, f32[256,448]{1,0:T(8,128)}, u32[]{:S(2)}) copy-start(f32[256,448]{1,0:T(8,128)} %get-tuple-element.83) | copy-start | bytes 1376260
  136.9 1.2 copy-start.5
  136.9 2.4 %copy-start.12 = (bf16[2,2048,448]{1,2,0:T(8,128)(2,1)S(1)}, bf16[2,2048,448]{1,2,0:T(8,128)(2,1)}, u32[]{:S(2)}) copy-start(bf16[2,2048,448]{1,2,0:T(8,128)(2,1)} %param.9) | copy-start | bytes 11010052
  139.3 2.0 copy-start.9
  141.3 1.2 copy-start.2
  142.5 27.8 %copy-start.20 = (f32[256,448]{1,0:T(8,128)S(1)}, f32[256,448]{1,0:T(8,128)}, u32[]{:S(2)}) copy-start(f32[256,448]{1,0:T(8,128)} %copy-done.19) | copy-start | bytes 1376260
  142.5 27.9 %copy-start.23 = (f32[256,448]{1,0:T(8,128)S(1)}, f32[256,448]{1,0:T(8,128)}, u32[]{:S(2)}) copy-start(f32[256,448]{1,0:T(8,128)} %copy-done.22) | copy-start | bytes 1376260

commit v4 on v3

--- a/solution.py
+++ b/solution.py
@@ -410,7 +410,7 @@
 
         def piece(step, carry):
             span = pl.ds(pl.multiple_of(step * chunk, chunk), chunk)
-            value, grad = rights[k % 3][k // 3, span], helds[k % 3][k // 3, span]
+            value, grad = rights[k % 3][k // 3, span], helds[k % 3][k // 3, span].astype(jnp.float32)
             return carry[0] + folded(value * grad), carry[1] + folded(grad * grad)
 
         sums = lax.fori_loop(0, rows // chunk, piece, sums)
@@ -449,7 +449,8 @@
     out, *kept = pl.pallas_call(
         functools.partial(scalar_kernel, dp, mp, scale),
         out_shape=[jax.ShapeDtypeStruct((8, 128), jnp.float32)]
-        + [pltpu.VMEM((2, hidden, width), jnp.float32)] * 6,
+        + [pltpu.VMEM((2, hidden, width), jnp.float32)] * 3
+        + [pltpu.VMEM((2, hidden, width), jnp.bfloat16)] * 3,
         in_specs=[vmem, vmem] + [anywhere] * 9,
         out_specs=[vmem] * 7,
         scratch_shapes=[
@@ -478,7 +479,7 @@
             span = pl.ds(pl.multiple_of(step * chunk, chunk), chunk)
             value = rights[which][layer, span]
             steps[k, span] = alpha * value
-            nexts[k, span] = keep * value - drop * helds[which][layer, span]
+            nexts[k, span] = keep * value - drop * helds[which][layer, span].astype(jnp.float32)
             return carry
 
         lax.fori_loop(0, rows // chunk, piece, 0)
@@ -583,7 +584,8 @@
     gates, ups, backs = swapped((back_gate, back_up), (back_layer,), 5)
     first = (rows_product(gates, inputs), rows_product(ups, inputs), rows_product(first_hiddens, backs))
     factors, rights, helds = coefficients(
-        dp, mp, scale, norm, damping, turned, first + second, 4
+        dp, mp, scale, norm, damping, turned,
+        [grad.astype(jnp.bfloat16) for grad in first + second], 4
     )
     outs = finished(factors, rights, helds)
     steps, nexts = list(outs[:3]), list(outs[3:])

time: 215 us -> 205 us (0.953)
  matrix products: 41.3 us -> 33.9 us
  Pallas kernels: 159 us -> 156 us
    dot_general x6, matrix products: 11.4 us -> 3.96 us  [rows_product(): lax.dot_general(left, right, (((0,), (0,)), ((), ())), preferred_element_...]
    pallas_call x1, Pallas kernels: 20.6 us -> 17.7 us  [coefficients(): pl.pallas_call(functools.partial(scalar_kernel, dp, mp, scale), out_shape...]
where the time goes in v4:
time: 205 us; the launch traced here: 204 us
  Pallas kernels  156 us (76%)
  matrix products  33.9 us (17%)
  local copies, waits for them, and re-layouts  12.5 us (6%)
    pallas_call x3, Pallas kernels, summed_whole(): pl.pallas_call(functools.partial(sum_kernel, outer, inner, count, which,...  105 us
    dot_general x10, matrix products, matmul(): return jnp.dot(left, right, preferred_element_type=jnp.float32)  22.7 us
    pallas_call x1, Pallas kernels, gathered(): pl.pallas_call(functools.partial(gather_kernel, outer, inner), out_shape=...  22.6 us
    pallas_call x1, Pallas kernels, coefficients(): pl.pallas_call(functools.partial(scalar_kernel, dp, mp, scale), out_shape...  17.7 us
    unnamed x49, local copies, waits for them, and re-layouts  11.2 us
    pallas_call x1, Pallas kernels, finished(): pl.pallas_call(finish_kernel, out_shape=[pltpu.HBM(shape, jnp.float32)] *...  8.26 us
    dot_general x7, matrix products, against(): lax.dot_general(left, right, (((1,), (1,)), ((), ())), preferred_element_...  7.23 us

profile of v4, /device:TPU:0, one launch (start us, length us, event | category | flops | bytes accessed | tf_op | source)
XLA Modules:
  0.0 204.4 jit_solution(13647417454026522078)
XLA Ops:
  1.3 0.8 copy-done.3
  2.1 22.6 %shard_map.127 = (bf16[4,4,256,128]{3,2,1,0:T(8,128)(2,1)S(1)}, f32[8,1024]{1,0:T(8,128)S(1)}, bf16[448,2048]{1,0:T(8,128)(2,1)S(1)}, bf16[448,2048]{1,0:T(8,128...) custom-call(bf16[256,128]{1,0:T(8,128)(2,1)S(1)} %copy-done.3, ...), custom_call_target="tpu_custom_call" | custom-call | tf_op jit(solution)/shard_map/pallas_call | solution.py:357
  26.2 1.7 copy-done.7
  29.4 1.6 convolution_multiply_fusion.1
  30.9 4.6 %fusion.20 = f32[256,2048]{1,0:T(8,128)} fusion(bf16[2,448,2048]{2,1,0:T(8,128)(2,1)} %param.11, f32[256,448]{1,0:T(8,128)} %convolution_multiply_fusion.1, bf16[448,2048]{1,0:T(8,128)(2,1)S(1)} %get-tuple-element.43, f32[256,448]{1,0:T(8,128)} %copy-done.19, bf16[32,8,16,128]{3,2,1,0:T(8,128)(2,1)S(1)} %bitcast.152), kind=kOutput, calls=%fused_computation.30 | convolution fusion | flops 940326912 | bytes 7864320 | tf_op jit(solution)/shard_map/dot_general | solution.py:519
  35.5 3.0 %fusion = bf16[256,2048]{1,0:T(8,128)(2,1)S(1)} fusion(f32[256,2048]{1,0:T(8,128)} %fusion.20, bf16[256,448]{1,0:T(8,128)(2,1)S(1)} %get-tuple-element.80.refs_5_, bf16[448,2048]{1,0:T(8,128)(2,1)} %get-tuple-element.44), kind=kOutput, calls=%fused_computation.4 | convolution fusion | flops 470810624 | bytes 5210112 | tf_op jit(solution)/shard_map/dot_general | solution.py:519
  38.7 1.7 convolution_convert_fusion
  41.1 1.2 copy-done
  42.3 47.9 %shard_map.128 = (bf16[4,4,16,2048]{3,2,1,0:T(8,128)(2,1)S(1)}, bf16[4,4,16,2048]{3,2,1,0:T(8,128)(2,1)S(1)}) custom-call(bf16[4,4,16,2048]{3,2,1,0:T(8,128)(2,1)S(1)} %bitcast.136, bf16[4,4,16,2048]{3,2,1,0:T(8,128)(2,1)S(1)} %bitcast.130, bf16[4,4,16,2048]{3,2,1,0:T(8,128)(2,1)S(1)} %reshape_reshape.3.refs_2_), custom_call_target="tpu_custom_call" | custom-call | tf_op jit(solution)/shard_map/pallas_call | solution.py:223
  91.0 1.1 copy-done.15
  92.2 1.6 fusion.66
  95.1 1.3 copy-done.8
  96.4 1.6 fusion.52
  98.1 1.6 multiply_convert_fusion.4
  99.6 5.6 %fusion.5 = f32[256,2048]{1,0:T(8,128)} fusion(bf16[2,448,2048]{2,1,0:T(8,128)(2,1)} %param.11, f32[256,448]{1,0:T(8,128)} %fusion.52, f32[256,448]{1,0:T(8,128)} %fusion.66, bf16[256,2048]{1,0:T(8,128)(2,1)S(1)} %bitcast.135, bf16[2,2048,448]{1,2,0:T(8,128)(2,1)} %param.9, f32[256,448]{1,0:T(8,128)} %get-tuple-element.83, f32[256,448]{1,0:T(8,128)} %copy-done.17), kind=kOutput, calls=%fused_computation.15 | convolution fusion | flops 940900352 | bytes 8912896 | tf_op jit(solution)/shard_map/dot_general | solution.py:519
  105.3 2.5 %fusion.1 = bf16[256,2048]{1,0:T(8,128)(2,1)S(1)} fusion(f32[256,2048]{1,0:T(8,128)} %fusion.5, bf16[256,448]{1,0:T(8,128)(2,1)S(1)} %get-tuple-element.82.refs_4_, bf16[448,2048]{1,0:T(8,128)(2,1)S(1)} %copy-done.6), kind=kOutput, calls=%fused_computation.5 | convolution fusion | flops 470810624 | bytes 5210112 | tf_op jit(solution)/shard_map/dot_general | solution.py:519
  107.7 29.1 %shard_map.129.refs_1_ = bf16[4,4,16,2048]{3,2,1,0:T(8,128)(2,1)S(1)} custom-call(bf16[4,4,16,2048]{3,2,1,0:T(8,128)(2,1)S(1)} %bitcast.131, bf16[4,4,16,2048]{3,2,1,0:T(8,128)(2,1)S(1)} %get-tuple-element.46.refs_1_), custom_call_target="tpu_custom_call" | custom-call | tf_op jit(solution)/shard_map/pallas_call | solution.py:223
  138.4 0.9 copy-done.12
  140.0 1.3 copy-done.9
  142.5 27.8 %shard_map.130 = (bf16[4,4,16,2048]{3,2,1,0:T(8,128)(2,1)S(1)}, bf16[2,256,448]{2,1,0:T(8,128)(2,1)S(1)}, bf16[2,256,448]{2,1,0:T(8,128)(2,1)S(1)}, bf16[2,256,4...) custom-call(bf16[4,4,16,2048]{3,2,1,0:T(8,128)(2,1)S(1)} %bitcast.13, ...), custom_call_target="tpu_custom_call" | custom-call | tf_op jit(solution)/shard_map/pallas_call | solution.py:223
  170.4 1.1 multiply_convert_fusion
  171.5 2.7 %shard_map.131 = (bf16[2,256,448]{2,1,0:T(8,128)(2,1)S(1)}, bf16[2,256,448]{2,1,0:T(8,128)(2,1)S(1)}, bf16[2,256,1024]{2,1,0:T(8,128)(2,1)S(1)}) custom-call(bf16[256,448]{1,0:T(8,128)(2,1)S(1)} %get-tuple-element.75.refs_0_, bf16[256,448]{1,0:T(8,128)(2,1)S(1)} %get-tuple-element.74.refs_1_, bf16[256,2048]{1,0:T(8,128)(2,1)S(1)} %bitcast.138), custom_call_target="tpu_custom_call" | custom-call | tf_op jit(solution)/shard_map/pallas_call | solution.py:262
  178.2 17.7 %shard_map.132 = (f32[8,128]{1,0:T(8,128)S(1)}, f32[2,448,1024]{2,1,0:T(8,128)S(1)}, f32[2,448,1024]{2,1,0:T(8,128)S(1)}, f32[2,448,1024]{2,1,0:T(8,128)S(1)}, b...) custom-call(f32[8,1024]{1,0:T(8,128)S(1)} %get-tuple-element.40.norm, ...), custom_call_target="tpu_custom_call" | custom-call | tf_op jit(solution)/shard_map/pallas_call | solution.py:449
  195.9 8.3 %shard_map.133 = (f32[2,448,1024]{2,1,0:T(8,128)}, f32[2,448,1024]{2,1,0:T(8,128)}, f32[2,448,1024]{2,1,0:T(8,128)}, f32[2,448,1024]{2,1,0:T(8,128)}, f32[2,448,1024]{2,1,0:T(8,128)}, /*index=5*/f32[2,448,1024]{2,1,0:T(8,128)}) custom-call(f32[8,128]{1,0:T(8,128)S(1)} %get-tuple-element.61.factors, f32[2,448,1024]{2,1,0:T(8,128)S(1)} %get-tuple-element.62.refs_0_, ...), custom_call_target="tpu_custom_call" | custom-call | tf_op jit(solution)/shard_map/pallas_call | solution.py:499
  (57 shorter events, 13.4 us)
Async XLA Ops:
  1.3 0.8 copy-start.3
  2.1 23.3 %copy-start.10 = (bf16[2,2048,448]{1,2,0:T(8,128)(2,1)S(1)}, bf16[2,2048,448]{1,2,0:T(8,128)(2,1)}, u32[]{:S(2)}) copy-start(bf16[2,2048,448]{1,2,0:T(8,128)(2,1)} %param.9) | copy-start | bytes 11010052
  25.4 15.0 %copy-start.4 = (bf16[16,256,128]{2,0,1:T(8,128)(2,1)}, bf16[16,256,128]{2,0,1:T(8,128)(2,1)S(1)}, u32[]{:S(2)}) copy-start(bf16[16,256,128]{2,0,1:T(8,128)(2,1)S(1)} %copy.61) | copy-start | bytes 3145732
  25.4 2.4 %copy-start.7 = (bf16[2,2048,448]{1,2,0:T(8,128)(2,1)S(1)}, bf16[2,2048,448]{1,2,0:T(8,128)(2,1)}, u32[]{:S(2)}) copy-start(bf16[2,2048,448]{1,2,0:T(8,128)(2,1)} %param.10) | copy-start | bytes 11010052
  27.8 0.8 copy-start.19
  28.6 0.8 copy-start.22
  35.5 3.2 %copy-start.13 = (bf16[2,448,2048]{2,1,0:T(8,128)(2,1)S(1)}, bf16[2,448,2048]{2,1,0:T(8,128)(2,1)}, u32[]{:S(2)}) copy-start(bf16[2,448,2048]{2,1,0:T(8,128)(2,1)} %param.11) | copy-start | bytes 11010052
  41.1 1.2 copy-start
  42.3 48.0 %copy-start.16 = (bf16[448,2048]{1,0:T(8,128)(2,1)S(1)}, bf16[448,2048]{1,0:T(8,128)(2,1)}, u32[]{:S(2)}) copy-start(bf16[448,2048]{1,0:T(8,128)(2,1)} %get-tuple-element.48) | copy-start | bytes 5505028
  90.3 7.8 %copy-start.1 = (bf16[4,4,16,2048]{3,2,1,0:T(8,128)(2,1)}, bf16[4,4,16,2048]{3,2,1,0:T(8,128)(2,1)S(1)}, u32[]{:S(2)}) copy-start(bf16[4,4,16,2048]{3,2,1,0:T(8,128)(2,1)S(1)} %get-tuple-element.45) | copy-start | bytes 3145732
  90.3 1.9 copy-start.15
  92.2 2.2 %copy-start.11 = (bf16[2,2048,448]{1,2,0:T(8,128)(2,1)S(1)}, bf16[2,2048,448]{1,2,0:T(8,128)(2,1)}, u32[]{:S(2)}) copy-start(bf16[2,2048,448]{1,2,0:T(8,128)(2,1)} %param.9) | copy-start | bytes 11010052
  94.4 2.0 copy-start.8
  96.4 1.6 copy-start.17
  99.6 5.6 %copy-start.6 = (bf16[448,2048]{1,0:T(8,128)(2,1)S(1)}, bf16[448,2048]{1,0:T(8,128)(2,1)}, u32[]{:S(2)}) copy-start(bf16[448,2048]{1,0:T(8,128)(2,1)} %get-tuple-element.49) | copy-start | bytes 5505028
  105.3 31.6 %copy-start.14 = (bf16[2,448,2048]{2,1,0:T(8,128)(2,1)S(1)}, bf16[2,448,2048]{2,1,0:T(8,128)(2,1)}, u32[]{:S(2)}) copy-start(bf16[2,448,2048]{2,1,0:T(8,128)(2,1)} %param.11) | copy-start | bytes 11010052
  107.7 29.2 %copy-start.18 = (f32[256,448]{1,0:T(8,128)S(1)}, f32[256,448]{1,0:T(8,128)}, u32[]{:S(2)}) copy-start(f32[256,448]{1,0:T(8,128)} %copy-done.17) | copy-start | bytes 1376260
  107.7 29.2 %copy-start.21 = (f32[256,448]{1,0:T(8,128)S(1)}, f32[256,448]{1,0:T(8,128)}, u32[]{:S(2)}) copy-start(f32[256,448]{1,0:T(8,128)} %get-tuple-element.83) | copy-start | bytes 1376260
  136.9 1.2 copy-start.5
  136.9 2.4 %copy-start.12 = (bf16[2,2048,448]{1,2,0:T(8,128)(2,1)S(1)}, bf16[2,2048,448]{1,2,0:T(8,128)(2,1)}, u32[]{:S(2)}) copy-start(bf16[2,2048,448]{1,2,0:T(8,128)(2,1)} %param.9) | copy-start | bytes 11010052
  139.3 2.0 copy-start.9
  141.3 1.2 copy-start.2
  142.5 27.8 %copy-start.20 = (f32[256,448]{1,0:T(8,128)S(1)}, f32[256,448]{1,0:T(8,128)}, u32[]{:S(2)}) copy-start(f32[256,448]{1,0:T(8,128)} %copy-done.19) | copy-start | bytes 1376260
  142.5 27.9 %copy-start.23 = (f32[256,448]{1,0:T(8,128)S(1)}, f32[256,448]{1,0:T(8,128)}, u32[]{:S(2)}) copy-start(f32[256,448]{1,0:T(8,128)} %copy-done.22) | copy-start | bytes 1376260
